TPU v7x, 256 devices: a whole 4x4x8 slice. The times are simulated.
256 devices in a mesh: seq: 256 (over x, z, y, core).
Axes of the slice: x: 4, y: 4, z: 8, core: 2. Of those that a mesh axis runs over, the one named last changes fastest.
Arguments:
- queries: bfloat16 [65536, 8, 128], P('seq'), may hold values from -6 to 6
- key_rows: bfloat16 [65536, 4, 128], P('seq'), may hold values from -6 to 6
- value_rows: bfloat16 [65536, 4, 128], P('seq'), may hold values from -6 to 6
- attn_output: bfloat16 [65536, 8, 128], P('seq'), may hold values from -6 to 6
- grad_output: bfloat16 [65536, 8, 128], P('seq'), may hold values from -144 to 144
- log_norm: float32 [8, 65536], P(None, 'seq'), may hold values from 6.5 to 8
Outputs:
- grad_queries: bfloat16 [65536, 8, 128], P('seq')
- grad_keys: bfloat16 [65536, 4, 128], P('seq')
- grad_values: bfloat16 [65536, 4, 128], P('seq')
All inputs are finite; a program needn't handle non-finite values.
Results may differ from a plain program's by a relative error of at most 0.0057.
Values may be sent and summed in bfloat16 or wider, within the bound.
A program may use at most 64 MiB of HBM per device.

v0:
```python
import jax
import jax.numpy as jnp
from jax import lax
from jax.sharding import PartitionSpec as P

W = 1024


query_scale = 168.0 ** (-0.5)


def from_behind(block, axis, distance):
    devices = range(lax.axis_size(axis))
    route = [(i - distance, i) for i in devices if i - distance in devices]
    return lax.ppermute(block, axis, route)


def band_mask(query_pos, key_pos, seq_rows):
    offset = query_pos[:, None] - key_pos[None, :]
    inside = (offset >= 0) & (offset < W)
    return inside & (key_pos >= 0)[None, :] & (query_pos < seq_rows)[:, None]


def band_grads(queries, grad_output, log_norm, delta_rows, key_rows, value_rows, allowed):
    row_count, head_count, head_size = queries.shape
    group_count = key_rows.shape[1]
    share = head_count // group_count
    query_group = queries.reshape(row_count, group_count, share, head_size)
    grad_group = grad_output.reshape(row_count, group_count, share, head_size)
    scores = (
        jnp.einsum("qkgd,lkd->kgql", query_group, key_rows, preferred_element_type=jnp.float32)
        * query_scale
    )
    norm_part = log_norm.reshape(group_count, share, row_count)[..., None]
    delta_part = delta_rows.reshape(group_count, share, row_count)[..., None]
    probs = jnp.where(allowed[None, None], jnp.exp(scores - norm_part), 0.0)
    grad_v = jnp.einsum(
        "kgql,qkgd->lkd", probs.astype(jnp.bfloat16), grad_group, preferred_element_type=jnp.float32
    )
    dprobs = jnp.einsum(
        "qkgd,lkd->kgql", grad_group, value_rows, preferred_element_type=jnp.float32
    )
    dscores = (probs * (dprobs - delta_part)).astype(jnp.bfloat16)
    grad_q = (
        jnp.einsum("kgql,lkd->qkgd", dscores, key_rows, preferred_element_type=jnp.float32)
        * query_scale
    )
    grad_k = (
        jnp.einsum("kgql,qkgd->lkd", dscores, query_group, preferred_element_type=jnp.float32)
        * query_scale
    )
    return (grad_q.reshape(row_count, head_count, head_size), grad_k, grad_v)


def shards(queries, key_rows, value_rows, attn_output, grad_output, log_norm):
    local_rows = queries.shape[0]
    hop_count = W // local_rows
    row_block = min(local_rows, 256)
    device = lax.axis_index("seq")
    seq_rows = lax.axis_size("seq") * local_rows
    own_first = device * local_rows
    ext_first = own_first - W
    delta_rows = jnp.sum(
        grad_output.astype(jnp.float32) * attn_output.astype(jnp.float32), axis=-1
    ).T
    halo_parts = []
    for distance in range(1, hop_count + 1):
        halo_parts.append(from_behind((key_rows, value_rows), "seq", distance))
    ordered = halo_parts[::-1]
    ext_keys = jnp.concatenate([pair_part[0] for pair_part in ordered] + [key_rows], 0)
    ext_values = jnp.concatenate([pair_part[1] for pair_part in ordered] + [value_rows], 0)

    def sweep(bounds):
        ext_grad_k = jnp.zeros(ext_keys.shape, jnp.float32)
        ext_grad_v = jnp.zeros(ext_keys.shape, jnp.float32)
        key_low, key_high = bounds[0]
        allowed = band_mask(
            own_first + 0 + jnp.arange(row_block, dtype=jnp.int32),
            ext_first + key_low + jnp.arange(key_high - key_low, dtype=jnp.int32),
            seq_rows,
        )
        grad_q, grad_k, grad_v = band_grads(
            queries,
            grad_output,
            log_norm,
            delta_rows,
            ext_keys[key_low:key_high],
            ext_values[key_low:key_high],
            allowed,
        )
        ext_grad_k = ext_grad_k.at[key_low:key_high].add(grad_k)
        ext_grad_v = ext_grad_v.at[key_low:key_high].add(grad_v)
        return (grad_q, ext_grad_k, ext_grad_v)

    halo_bounds = [(0, W)]
    local_bounds = [(W, W + row_block)]
    grad_halo, halo_k, halo_v = sweep(halo_bounds)
    deliver_halo_k = halo_k[:W]
    deliver_halo_v = halo_v[:W]
    taken_k = jnp.zeros(key_rows.shape, jnp.float32)
    taken_v = jnp.zeros(key_rows.shape, jnp.float32)
    for distance in range(1, hop_count + 1):
        lower = (hop_count - distance) * local_rows
        got_k, got_v = from_behind(
            (
                deliver_halo_k[lower : lower + local_rows].astype(jnp.bfloat16),
                deliver_halo_v[lower : lower + local_rows].astype(jnp.bfloat16),
            ),
            "seq",
            -distance,
        )
        taken_k = taken_k + got_k.astype(jnp.float32)
        taken_v = taken_v + got_v.astype(jnp.float32)
    taken_k, taken_v = (taken_k, taken_v)
    grad_local, local_k, local_v = sweep(local_bounds)
    grad_total = grad_halo + grad_local
    own_k = local_k[W:] + taken_k
    own_v = local_v[W:] + taken_v
    return (grad_total.astype(jnp.bfloat16), own_k.astype(jnp.bfloat16), own_v.astype(jnp.bfloat16))


def solution(mesh):
    in_specs = (
        P("seq", None, None),
        P("seq", None, None),
        P("seq", None, None),
        P("seq", None, None),
        P("seq", None, None),
        P(None, "seq"),
    )
    out_specs = (P("seq", None, None), P("seq", None, None), P("seq", None, None))
    return jax.shard_map(shards, mesh=mesh, in_specs=in_specs, out_specs=out_specs, check_vma=False)
```

profile of v0, /device:TPU:6, one launch (start us, length us, event | category | flops | bytes accessed | tf_op | source)
XLA Modules:
  0.0 98.1 jit_solution(2786235913290026084)
XLA Ops:
  2.4 5.1 %collective-permute-start = (bf16[256,4,128]{2,0,1:T(8,128)(2,1)}, bf16[256,4,128]{2,0,1:T(8,128)(2,1)}, u32[]{:S(2)}, u32[]{:S(2)}) collective-permute-start(bf16[256,4,128]{2,0,1:T(8,128)(2,1)} %copy.63), channel_id=1, source_target_pairs={{0,4},{1,5},{2,6},{3,7},{4,8},{5,9},{6,10},{7,11},{8,12},{9,13},{1... | collective-permute-start | bytes 786440 | tf_op jit(solution)/shard_map/ppermute | solution.py:15
  7.5 1.9 %collective-permute-start.1 = (bf16[256,4,128]{2,0,1:T(8,128)(2,1)}, bf16[256,4,128]{2,0,1:T(8,128)(2,1)}, u32[]{:S(2)}, u32[]{:S(2)}) collective-permute-start(bf16[256,4,128]{2,0,1:T(8,128)(2,1)} %copy.63), channel_id=1, source_target_pairs={{0,3},{1,4},{2,5},{3,6},{4,7},{5,8},{6,9},{7,10},{8,11},{9,12},{10... | collective-permute-start | bytes 786440 | tf_op jit(solution)/shard_map/ppermute | solution.py:15
  9.4 2.7 %collective-permute-start.2 = (bf16[256,4,128]{2,0,1:T(8,128)(2,1)}, bf16[256,4,128]{2,0,1:T(8,128)(2,1)}, u32[]{:S(2)}, u32[]{:S(2)}) collective-permute-start(bf16[256,4,128]{2,0,1:T(8,128)(2,1)} %copy.63), channel_id=1, source_target_pairs={{0,2},{1,3},{2,4},{3,5},{4,6},{5,7},{6,8},{7,9},{8,10},{9,11},{10,... | collective-permute-start | bytes 786440 | tf_op jit(solution)/shard_map/ppermute | solution.py:15
  12.2 4.2 %collective-permute-start.3 = (bf16[256,4,128]{2,0,1:T(8,128)(2,1)}, bf16[256,4,128]{2,0,1:T(8,128)(2,1)}, u32[]{:S(2)}, u32[]{:S(2)}) collective-permute-start(bf16[256,4,128]{2,0,1:T(8,128)(2,1)} %copy.63), channel_id=1, source_target_pairs={{0,1},{1,2},{2,3},{3,4},{4,5},{5,6},{6,7},{7,8},{8,9},{9,10},{10,1... | collective-permute-start | bytes 786440 | tf_op jit(solution)/shard_map/ppermute | solution.py:15
  18.1 4.8 %collective-permute-start.4 = (bf16[256,4,128]{2,0,1:T(8,128)(2,1)}, bf16[256,4,128]{2,0,1:T(8,128)(2,1)}, u32[]{:S(2)}, u32[]{:S(2)}) collective-permute-start(bf16[256,4,128]{2,0,1:T(8,128)(2,1)} %copy.68), channel_id=1, source_target_pairs={{0,4},{1,5},{2,6},{3,7},{4,8},{5,9},{6,10},{7,11},{8,12},{9,13},{1... | collective-permute-start | bytes 786440 | tf_op jit(solution)/shard_map/ppermute | solution.py:15
  28.7 2.2 %collective-permute-start.5 = (bf16[256,4,128]{2,0,1:T(8,128)(2,1)}, bf16[256,4,128]{2,0,1:T(8,128)(2,1)S(1)}, u32[]{:S(2)}, u32[]{:S(2)}) collective-permute-start(bf16[256,4,128]{2,0,1:T(8,128)(2,1)} %copy.68), channel_id=1, source_target_pairs={{0,3},{1,4},{2,5},{3,6},{4,7},{5,8},{6,9},{7,10},{8,11},{9,12},{10... | collective-permute-start | bytes 786440 | tf_op jit(solution)/shard_map/ppermute | solution.py:15
  31.0 2.9 %collective-permute-start.6 = (bf16[256,4,128]{2,0,1:T(8,128)(2,1)}, bf16[256,4,128]{2,0,1:T(8,128)(2,1)S(1)}, u32[]{:S(2)}, u32[]{:S(2)}) collective-permute-start(bf16[256,4,128]{2,0,1:T(8,128)(2,1)} %copy.68), channel_id=1, source_target_pairs={{0,2},{1,3},{2,4},{3,5},{4,6},{5,7},{6,8},{7,9},{8,10},{9,11},{10,... | collective-permute-start | bytes 786440 | tf_op jit(solution)/shard_map/ppermute | solution.py:15
  33.8 2.7 %collective-permute-done.2 = bf16[256,4,128]{2,0,1:T(8,128)(2,1)} collective-permute-done((bf16[256,4,128]{2,0,1:T(8,128)(2,1)}, bf16[256,4,128]{2,0,1:T(8,128)(2,1)}, u32[]{:S(2)}, u32[]{:S(2)}) %collective-permute-start.2) | collective-permute-done | bytes 262176 | tf_op jit(solution)/shard_map/ppermute | solution.py:15
  36.5 1.9 %collective-permute-start.7 = (bf16[256,4,128]{2,0,1:T(8,128)(2,1)}, bf16[256,4,128]{2,0,1:T(8,128)(2,1)S(1)}, u32[]{:S(2)}, u32[]{:S(2)}) collective-permute-start(bf16[256,4,128]{2,0,1:T(8,128)(2,1)} %copy.68), channel_id=1, source_target_pairs={{0,1},{1,2},{2,3},{3,4},{4,5},{5,6},{6,7},{7,8},{8,9},{9,10},{10,1... | collective-permute-start | bytes 786440 | tf_op jit(solution)/shard_map/ppermute | solution.py:15
  38.5 1.9 %collective-permute-done.3 = bf16[256,4,128]{2,0,1:T(8,128)(2,1)} collective-permute-done((bf16[256,4,128]{2,0,1:T(8,128)(2,1)}, bf16[256,4,128]{2,0,1:T(8,128)(2,1)}, u32[]{:S(2)}, u32[]{:S(2)}) %collective-permute-start.3) | collective-permute-done | bytes 262176 | tf_op jit(solution)/shard_map/ppermute | solution.py:15
  40.4 2.4 %fusion.38 = f32[4,1024,256,2]{2,1,3,0:T(8,128)S(1)} fusion(bf16[256,4,128]{2,0,1:T(8,128)(2,1)} %collective-permute-done.3, bf16[256,4,128]{2,0,1:T(8,128)(2,1)} %collective-permute-done.2, bf16[256,4,128]{2,0,1:T(8,128)(2,1)} %collective-permute-done.1, bf16[256,4,128]{2,0,1:T(8,128)(2,1)} %collective-permute-done, bf16[256,4,2,128]{3,2,1,0:T(2,128)(2,1)S(1)} %bitcast.102), kind=kOutput, calls=%fused_computation.50 | convolution fusion | flops 541065216 | bytes 9961472 | tf_op jit(solution)/shard_map/qkgd,lkd->kgql/dot_general | solution.py:31
  45.4 5.9 %collective-permute-start.12 = (bf16[256,4,128]{2,0,1:T(8,128)(2,1)}, bf16[256,4,128]{2,0,1:T(8,128)(2,1)}, u32[]{:S(2)}, u32[]{:S(2)}) collective-permute-start(bf16[256,4,128]{2,0,1:T(8,128)(2,1)} %get-tuple-element.60), channel_id=1, source_target_pairs={{1,0},{2,1},{3,2},{4,3},{5,4},{6,5},{7,6},{8,7},{9,8},{10,9},{11,1... | collective-permute-start | bytes 786440 | tf_op jit(solution)/shard_map/ppermute | solution.py:15
  51.3 3.6 %collective-permute-start.13 = (bf16[256,4,128]{2,0,1:T(8,128)(2,1)}, bf16[256,4,128]{2,0,1:T(8,128)(2,1)}, u32[]{:S(2)}, u32[]{:S(2)}) collective-permute-start(bf16[256,4,128]{2,0,1:T(8,128)(2,1)} %get-tuple-element.63), channel_id=1, source_target_pairs={{2,0},{3,1},{4,2},{5,3},{6,4},{7,5},{8,6},{9,7},{10,8},{11,9},{12,... | collective-permute-start | bytes 786440 | tf_op jit(solution)/shard_map/ppermute | solution.py:15
  54.9 1.9 %collective-permute-start.14 = (bf16[256,4,128]{2,0,1:T(8,128)(2,1)}, bf16[256,4,128]{2,0,1:T(8,128)(2,1)}, u32[]{:S(2)}, u32[]{:S(2)}) collective-permute-start(bf16[256,4,128]{2,0,1:T(8,128)(2,1)} %get-tuple-element.62), channel_id=1, source_target_pairs={{3,0},{4,1},{5,2},{6,3},{7,4},{8,5},{9,6},{10,7},{11,8},{12,9},{13... | collective-permute-start | bytes 786440 | tf_op jit(solution)/shard_map/ppermute | solution.py:15
  56.9 3.1 %collective-permute-start.15 = (bf16[256,4,128]{2,0,1:T(8,128)(2,1)S(1)}, bf16[256,4,128]{2,0,1:T(8,128)(2,1)}, u32[]{:S(2)}, u32[]{:S(2)}) collective-permute-start(bf16[256,4,128]{2,0,1:T(8,128)(2,1)S(1)} %get-tuple-element.61), channel_id=1, source_target_pairs={{4,0},{5,1},{6,2},{7,3},{8,4},{9,5},{10,6},{11,7},{12,8},{13,9},{1... | collective-permute-start | bytes 786440 | tf_op jit(solution)/shard_map/ppermute | solution.py:15
  60.0 3.7 %fusion.1 = bf16[4,2,256,1024]{2,3,1,0:T(8,128)(2,1)S(1)} fusion(f32[4,1024,256,2]{2,1,3,0:T(8,128)S(1)} %fusion.38, f32[4,2,256]{2,1,0:T(2,128)S(1)} %sub.80, f32[4,2,256]{2,1,0:T(2,128)S(1)} %sub.77, pred[256,1024]{0,1:T(8,128)(4,1)S(1)} %fusion.37, bf16[256,4,128]{2,0,1:T(8,128)(2,1)S(1)} %collective-permute-done.7, ...), kind=kOutput, calls=%fused_computation.2 | convolution fusion | flops 553648128 | bytes 14434304 | tf_op jit(solution)/shard_map/qkgd,lkd->kgql/dot_general | solution.py:40
  65.9 2.7 %collective-permute-start.10 = (bf16[256,4,128]{2,0,1:T(8,128)(2,1)}, bf16[256,4,128]{2,0,1:T(8,128)(2,1)}, u32[]{:S(2)}, u32[]{:S(2)}) collective-permute-start(bf16[256,4,128]{2,0,1:T(8,128)(2,1)} %get-tuple-element.66), channel_id=1, source_target_pairs={{3,0},{4,1},{5,2},{6,3},{7,4},{8,5},{9,6},{10,7},{11,8},{12,9},{13... | collective-permute-start | bytes 786440 | tf_op jit(solution)/shard_map/ppermute | solution.py:15
  68.6 2.8 %fusion.25 = bf16[256,4,2,128]{0,3,2,1:T(8,128)(2,1)} fusion(f32[256,4,2,128]{0,3,2,1:T(8,128)S(1)} %fusion.24, bf16[4,2,256,1024]{2,3,1,0:T(8,128)(2,1)S(1)} %fusion.1, bf16[256,4,128]{2,0,1:T(8,128)(2,1)} %collective-permute-done.3, bf16[256,4,128]{2,0,1:T(8,128)(2,1)} %collective-permute-done.2, bf16[256,4,128]{2,0,1:T(8,128)(2,1)} %collective-permute-done.1, ...), kind=kOutput, calls=%fused_computation.30 | convolution fusion | flops 541851648 | bytes 6815744 | tf_op jit(solution)/shard_map/kgql,lkd->qkgd/dot_general | solution.py:45
  71.5 2.1 %copy.87 = bf16[256,8,128]{2,1,0:T(8,128)(2,1)} copy(bf16[256,8,128]{0,2,1:T(8,128)(2,1)} %bitcast.114) | data formatting | bytes 1048576
  73.6 4.6 %collective-permute-start.11 = (bf16[256,4,128]{2,0,1:T(8,128)(2,1)}, bf16[256,4,128]{2,0,1:T(8,128)(2,1)S(1)}, u32[]{:S(2)}, u32[]{:S(2)}) collective-permute-start(bf16[256,4,128]{2,0,1:T(8,128)(2,1)} %get-tuple-element.65), channel_id=1, source_target_pairs={{4,0},{5,1},{6,2},{7,3},{8,4},{9,5},{10,6},{11,7},{12,8},{13,9},{1... | collective-permute-start | bytes 786440 | tf_op jit(solution)/shard_map/ppermute | solution.py:15
  78.2 2.4 %collective-permute-start.8 = (bf16[256,4,128]{2,0,1:T(8,128)(2,1)}, bf16[256,4,128]{2,0,1:T(8,128)(2,1)S(1)}, u32[]{:S(2)}, u32[]{:S(2)}) collective-permute-start(bf16[256,4,128]{2,0,1:T(8,128)(2,1)} %get-tuple-element.64), channel_id=1, source_target_pairs={{1,0},{2,1},{3,2},{4,3},{5,4},{6,5},{7,6},{8,7},{9,8},{10,9},{11,1... | collective-permute-start | bytes 786440 | tf_op jit(solution)/shard_map/ppermute | solution.py:15
  80.6 4.0 %collective-permute-start.9 = (bf16[256,4,128]{2,0,1:T(8,128)(2,1)}, bf16[256,4,128]{2,0,1:T(8,128)(2,1)S(1)}, u32[]{:S(2)}, u32[]{:S(2)}) collective-permute-start(bf16[256,4,128]{2,0,1:T(8,128)(2,1)} %get-tuple-element.67), channel_id=1, source_target_pairs={{2,0},{3,1},{4,2},{5,3},{6,4},{7,5},{8,6},{9,7},{10,8},{11,9},{12,... | collective-permute-start | bytes 786440 | tf_op jit(solution)/shard_map/ppermute | solution.py:15
  88.8 4.2 %collective-permute-done.8 = bf16[256,4,128]{2,0,1:T(8,128)(2,1)S(1)} collective-permute-done((bf16[256,4,128]{2,0,1:T(8,128)(2,1)}, bf16[256,4,128]{2,0,1:T(8,128)(2,1)S(1)}, u32[]{:S(2)}, u32[]{:S(2)}) %collective-permute-start.8) | collective-permute-done | bytes 262176 | tf_op jit(solution)/shard_map/ppermute | solution.py:15
  93.0 2.8 %collective-permute-done.9 = bf16[256,4,128]{2,0,1:T(8,128)(2,1)S(1)} collective-permute-done((bf16[256,4,128]{2,0,1:T(8,128)(2,1)}, bf16[256,4,128]{2,0,1:T(8,128)(2,1)S(1)}, u32[]{:S(2)}, u32[]{:S(2)}) %collective-permute-start.9) | collective-permute-done | bytes 262176 | tf_op jit(solution)/shard_map/ppermute | solution.py:15
  (46 shorter events, 20.4 us)
Async XLA Ops:
  0.6 25.7 %copy-start = (bf16[256,8,128]{2,1,0:T(8,128)(2,1)S(1)}, bf16[256,8,128]{2,1,0:T(8,128)(2,1)}, u32[]{:S(2)}) copy-start(bf16[256,8,128]{2,1,0:T(8,128)(2,1)} %param.14) | copy-start | bytes 1572868
  0.6 25.7 %copy-start.4 = (bf16[256,4,128]{2,1,0:T(4,128)(2,1)S(1)}, bf16[256,4,128]{2,1,0:T(4,128)(2,1)}, u32[]{:S(2)}) copy-start(bf16[256,4,128]{2,1,0:T(4,128)(2,1)} %param.15) | copy-start | bytes 786436
  2.4 26.3 %collective-permute-start = (bf16[256,4,128]{2,0,1:T(8,128)(2,1)}, bf16[256,4,128]{2,0,1:T(8,128)(2,1)}, u32[]{:S(2)}, u32[]{:S(2)}) collective-permute-start(bf16[256,4,128]{2,0,1:T(8,128)(2,1)} %copy.63), channel_id=1, source_target_pairs={{0,4},{1,5},{2,6},{3,7},{4,8},{5,9},{6,10},{7,11},{8,12},{9,13},{1... | collective-permute-start | bytes 786440 | tf_op jit(solution)/shard_map/ppermute | solution.py:15
  7.5 23.4 %collective-permute-start.1 = (bf16[256,4,128]{2,0,1:T(8,128)(2,1)}, bf16[256,4,128]{2,0,1:T(8,128)(2,1)}, u32[]{:S(2)}, u32[]{:S(2)}) collective-permute-start(bf16[256,4,128]{2,0,1:T(8,128)(2,1)} %copy.63), channel_id=1, source_target_pairs={{0,3},{1,4},{2,5},{3,6},{4,7},{5,8},{6,9},{7,10},{8,11},{9,12},{10... | collective-permute-start | bytes 786440 | tf_op jit(solution)/shard_map/ppermute | solution.py:15
  9.4 27.1 %collective-permute-start.2 = (bf16[256,4,128]{2,0,1:T(8,128)(2,1)}, bf16[256,4,128]{2,0,1:T(8,128)(2,1)}, u32[]{:S(2)}, u32[]{:S(2)}) collective-permute-start(bf16[256,4,128]{2,0,1:T(8,128)(2,1)} %copy.63), channel_id=1, source_target_pairs={{0,2},{1,3},{2,4},{3,5},{4,6},{5,7},{6,8},{7,9},{8,10},{9,11},{10,... | collective-permute-start | bytes 786440 | tf_op jit(solution)/shard_map/ppermute | solution.py:15
  12.2 28.2 %collective-permute-start.3 = (bf16[256,4,128]{2,0,1:T(8,128)(2,1)}, bf16[256,4,128]{2,0,1:T(8,128)(2,1)}, u32[]{:S(2)}, u32[]{:S(2)}) collective-permute-start(bf16[256,4,128]{2,0,1:T(8,128)(2,1)} %copy.63), channel_id=1, source_target_pairs={{0,1},{1,2},{2,3},{3,4},{4,5},{5,6},{6,7},{7,8},{8,9},{9,10},{10,1... | collective-permute-start | bytes 786440 | tf_op jit(solution)/shard_map/ppermute | solution.py:15
  18.1 33.3 %collective-permute-start.4 = (bf16[256,4,128]{2,0,1:T(8,128)(2,1)}, bf16[256,4,128]{2,0,1:T(8,128)(2,1)}, u32[]{:S(2)}, u32[]{:S(2)}) collective-permute-start(bf16[256,4,128]{2,0,1:T(8,128)(2,1)} %copy.68), channel_id=1, source_target_pairs={{0,4},{1,5},{2,6},{3,7},{4,8},{5,9},{6,10},{7,11},{8,12},{9,13},{1... | collective-permute-start | bytes 786440 | tf_op jit(solution)/shard_map/ppermute | solution.py:15
  25.2 1.7 %copy-start.1 = (bf16[256,8,128]{2,1,0:T(8,128)(2,1)S(1)}, bf16[256,8,128]{2,1,0:T(8,128)(2,1)}, u32[]{:S(2)}) copy-start(bf16[256,8,128]{2,1,0:T(8,128)(2,1)} %param.18) | copy-start | bytes 1572868
  28.3 10.1 %copy-start.2 = (bf16[4,2,256,256]{2,3,1,0:T(8,128)(2,1)}, bf16[4,2,256,256]{2,3,1,0:T(8,128)(2,1)S(1)}, u32[]{:S(2)}) copy-start(bf16[4,2,256,256]{2,3,1,0:T(8,128)(2,1)S(1)} %fusion.13) | copy-start | bytes 3145732
  28.7 26.2 %collective-permute-start.5 = (bf16[256,4,128]{2,0,1:T(8,128)(2,1)}, bf16[256,4,128]{2,0,1:T(8,128)(2,1)S(1)}, u32[]{:S(2)}, u32[]{:S(2)}) collective-permute-start(bf16[256,4,128]{2,0,1:T(8,128)(2,1)} %copy.68), channel_id=1, source_target_pairs={{0,3},{1,4},{2,5},{3,6},{4,7},{5,8},{6,9},{7,10},{8,11},{9,12},{10... | collective-permute-start | bytes 786440 | tf_op jit(solution)/shard_map/ppermute | solution.py:15
  31.0 25.9 %collective-permute-start.6 = (bf16[256,4,128]{2,0,1:T(8,128)(2,1)}, bf16[256,4,128]{2,0,1:T(8,128)(2,1)S(1)}, u32[]{:S(2)}, u32[]{:S(2)}) collective-permute-start(bf16[256,4,128]{2,0,1:T(8,128)(2,1)} %copy.68), channel_id=1, source_target_pairs={{0,2},{1,3},{2,4},{3,5},{4,6},{5,7},{6,8},{7,9},{8,10},{9,11},{10,... | collective-permute-start | bytes 786440 | tf_op jit(solution)/shard_map/ppermute | solution.py:15
  36.5 23.4 %collective-permute-start.7 = (bf16[256,4,128]{2,0,1:T(8,128)(2,1)}, bf16[256,4,128]{2,0,1:T(8,128)(2,1)S(1)}, u32[]{:S(2)}, u32[]{:S(2)}) collective-permute-start(bf16[256,4,128]{2,0,1:T(8,128)(2,1)} %copy.68), channel_id=1, source_target_pairs={{0,1},{1,2},{2,3},{3,4},{4,5},{5,6},{6,7},{7,8},{8,9},{9,10},{10,1... | collective-permute-start | bytes 786440 | tf_op jit(solution)/shard_map/ppermute | solution.py:15
  45.4 28.2 %collective-permute-start.12 = (bf16[256,4,128]{2,0,1:T(8,128)(2,1)}, bf16[256,4,128]{2,0,1:T(8,128)(2,1)}, u32[]{:S(2)}, u32[]{:S(2)}) collective-permute-start(bf16[256,4,128]{2,0,1:T(8,128)(2,1)} %get-tuple-element.60), channel_id=1, source_target_pairs={{1,0},{2,1},{3,2},{4,3},{5,4},{6,5},{7,6},{8,7},{9,8},{10,9},{11,1... | collective-permute-start | bytes 786440 | tf_op jit(solution)/shard_map/ppermute | solution.py:15
  51.3 26.8 %collective-permute-start.13 = (bf16[256,4,128]{2,0,1:T(8,128)(2,1)}, bf16[256,4,128]{2,0,1:T(8,128)(2,1)}, u32[]{:S(2)}, u32[]{:S(2)}) collective-permute-start(bf16[256,4,128]{2,0,1:T(8,128)(2,1)} %get-tuple-element.63), channel_id=1, source_target_pairs={{2,0},{3,1},{4,2},{5,3},{6,4},{7,5},{8,6},{9,7},{10,8},{11,9},{12,... | collective-permute-start | bytes 786440 | tf_op jit(solution)/shard_map/ppermute | solution.py:15
  54.9 25.7 %collective-permute-start.14 = (bf16[256,4,128]{2,0,1:T(8,128)(2,1)}, bf16[256,4,128]{2,0,1:T(8,128)(2,1)}, u32[]{:S(2)}, u32[]{:S(2)}) collective-permute-start(bf16[256,4,128]{2,0,1:T(8,128)(2,1)} %get-tuple-element.62), channel_id=1, source_target_pairs={{3,0},{4,1},{5,2},{6,3},{7,4},{8,5},{9,6},{10,7},{11,8},{12,9},{13... | collective-permute-start | bytes 786440 | tf_op jit(solution)/shard_map/ppermute | solution.py:15
  56.9 27.7 %collective-permute-start.15 = (bf16[256,4,128]{2,0,1:T(8,128)(2,1)S(1)}, bf16[256,4,128]{2,0,1:T(8,128)(2,1)}, u32[]{:S(2)}, u32[]{:S(2)}) collective-permute-start(bf16[256,4,128]{2,0,1:T(8,128)(2,1)S(1)} %get-tuple-element.61), channel_id=1, source_target_pairs={{4,0},{5,1},{6,2},{7,3},{8,4},{9,5},{10,6},{11,7},{12,8},{13,9},{1... | collective-permute-start | bytes 786440 | tf_op jit(solution)/shard_map/ppermute | solution.py:15
  65.9 21.2 %collective-permute-start.10 = (bf16[256,4,128]{2,0,1:T(8,128)(2,1)}, bf16[256,4,128]{2,0,1:T(8,128)(2,1)}, u32[]{:S(2)}, u32[]{:S(2)}) collective-permute-start(bf16[256,4,128]{2,0,1:T(8,128)(2,1)} %get-tuple-element.66), channel_id=1, source_target_pairs={{3,0},{4,1},{5,2},{6,3},{7,4},{8,5},{9,6},{10,7},{11,8},{12,9},{13... | collective-permute-start | bytes 786440 | tf_op jit(solution)/shard_map/ppermute | solution.py:15
  73.6 15.2 %collective-permute-start.11 = (bf16[256,4,128]{2,0,1:T(8,128)(2,1)}, bf16[256,4,128]{2,0,1:T(8,128)(2,1)S(1)}, u32[]{:S(2)}, u32[]{:S(2)}) collective-permute-start(bf16[256,4,128]{2,0,1:T(8,128)(2,1)} %get-tuple-element.65), channel_id=1, source_target_pairs={{4,0},{5,1},{6,2},{7,3},{8,4},{9,5},{10,6},{11,7},{12,8},{13,9},{1... | collective-permute-start | bytes 786440 | tf_op jit(solution)/shard_map/ppermute | solution.py:15
  78.2 14.8 %collective-permute-start.8 = (bf16[256,4,128]{2,0,1:T(8,128)(2,1)}, bf16[256,4,128]{2,0,1:T(8,128)(2,1)S(1)}, u32[]{:S(2)}, u32[]{:S(2)}) collective-permute-start(bf16[256,4,128]{2,0,1:T(8,128)(2,1)} %get-tuple-element.64), channel_id=1, source_target_pairs={{1,0},{2,1},{3,2},{4,3},{5,4},{6,5},{7,6},{8,7},{9,8},{10,9},{11,1... | collective-permute-start | bytes 786440 | tf_op jit(solution)/shard_map/ppermute | solution.py:15
  80.6 15.2 %copy-start.3 = (bf16[4,2,256,256]{2,3,1,0:T(8,128)(2,1)S(1)}, bf16[4,2,256,256]{2,3,1,0:T(8,128)(2,1)}, u32[]{:S(2)}) copy-start(bf16[4,2,256,256]{2,3,1,0:T(8,128)(2,1)} %copy-done.2) | copy-start | bytes 3145732
  80.6 15.2 %collective-permute-start.9 = (bf16[256,4,128]{2,0,1:T(8,128)(2,1)}, bf16[256,4,128]{2,0,1:T(8,128)(2,1)S(1)}, u32[]{:S(2)}, u32[]{:S(2)}) collective-permute-start(bf16[256,4,128]{2,0,1:T(8,128)(2,1)} %get-tuple-element.67), channel_id=1, source_target_pairs={{2,0},{3,1},{4,2},{5,3},{6,4},{7,5},{8,6},{9,7},{10,8},{11,9},{12,... | collective-permute-start | bytes 786440 | tf_op jit(solution)/shard_map/ppermute | solution.py:15
where the time goes:
time: 98.9 us; the launch traced here: 98.1 us
  starting transfers between devices  53.9 us (54%)
  matrix products  17.2 us (17%)
  waiting for transfers between devices  13.3 us (13%)
  local copies, waits for them, and re-layouts  10.1 us (10%)
  other arithmetic  2.56 us (3%)
  between operations  1.02 us (1%)
    ppermute x16, starting transfers between devices, from_behind(): return lax.ppermute(block, axis, route)  53.9 us
    ppermute x16, waiting for transfers between devices, from_behind(): return lax.ppermute(block, axis, route)  13.3 us
    unnamed x15, local copies, waits for them, and re-layouts  7.42 us
    dot_general x2, matrix products, band_grads(): jnp.einsum('qkgd,lkd->kgql', grad_group, value_rows, preferred_element_ty...  5.12 us
    dot_general x2, matrix products, band_grads(): jnp.einsum('kgql,qkgd->lkd', probs.astype(jnp.bfloat16), grad_group, pref...  3.26 us
    dot_general x2, matrix products, band_grads(): jnp.einsum('kgql,lkd->qkgd', dscores, key_rows, preferred_element_type=jn...  3.16 us
    dot_general x2, matrix products, band_grads(): jnp.einsum('qkgd,lkd->kgql', query_group, key_rows, preferred_element_typ...  3.06 us
    dot_general x2, matrix products, band_grads(): jnp.einsum('kgql,qkgd->lkd', dscores, query_group, preferred_element_type...  2.63 us
  transfers between devices with their start and end apart: 16, of which 5 were waited for; matrix products, arithmetic and copies ran while one was open for 26% of the time, Pallas kernels for 0%

commit v1 on v0

v1 whole, which is shorter than its diff:
```python
import functools
import math

import jax
import jax.numpy as jnp
from jax import lax
from jax.experimental import pallas as pl
from jax.experimental.pallas import tpu as pltpu
from jax.sharding import PartitionSpec as P

MESH = pl.DeviceIdType.MESH
BF = jnp.bfloat16
F32 = jnp.float32
SCALE = 168.0 ** (-0.5)
LOG2E = math.log2(math.e)
T = 256
HD = 128
NC = 4
TC = T // NC
NU = 2 * NC
FAR = 1e30


def dot_nt(a, b):
    return lax.dot_general(a, b, (((1,), (1,)), ((), ())), preferred_element_type=F32)


def dot_nn(a, b):
    return lax.dot_general(a, b, (((1,), (0,)), ((), ())), preferred_element_type=F32)


def dot_tn(a, b):
    return lax.dot_general(a, b, (((0,), (0,)), ((), ())), preferred_element_type=F32)


def kernel(
    n,
    q_hbm, k_hbm, v_hbm, o_hbm, g_hbm, lse_hbm,
    gq_out, gk_out, gv_out,
    kraw, kv_x, qb, gb, qx, gx, ob, lse_s, st, stx, kd, kf,
    acc_h, acc_l, acc_z, dq_t, dqs, g2s, g2r, g1s, g1r, g0r, fi, fo,
    kv_ld, in_ld,
    o_send, o_recv, r_send, r_recv, g2_send, g2_recv, g1_send, g1_recv,
    x_send, x_recv, dq_send, dq_recv, out_sem,
):
    me = lax.axis_index("seq")
    k = lax.rem(me, 2)
    oth = 1 - k
    chip = lax.div(me, 2)
    up = lax.rem(me - k + 2, n)
    down = lax.rem(me - k + n - 2, n)
    partner = me - k + oth

    def remote(src, dst, ssem, rsem, dev):
        return pltpu.make_async_remote_copy(
            src_ref=src, dst_ref=dst, send_sem=ssem, recv_sem=rsem,
            device_id=(dev,), device_id_type=MESH,
        )

    def par(u):
        return k if u % 2 == 0 else oth

    kv_loads = []
    for m in range(NC):
        rows = pl.ds(m * TC, TC)
        for i, (dst, pair) in enumerate(((kraw.at[4 + k, m], k), (kv_x.at[m], oth))):
            for e, src in enumerate((k_hbm, v_hbm)):
                kv_loads.append(
                    pltpu.make_async_copy(src.at[rows, pair], dst.at[e], kv_ld.at[m, i, e])
                )
    for c in kv_loads:
        c.start()
    in_loads = []
    s = 0
    for src, near, far in ((q_hbm, qb.at[k], qx), (g_hbm, gb.at[k], gx), (o_hbm, ob.at[0], ob.at[1])):
        for dst, base in ((near, k), (far, oth)):
            for j in range(2):
                in_loads.append(
                    pltpu.make_async_copy(src.at[:, 2 * base + j], dst.at[j], in_ld.at[s])
                )
                s += 1
    in_loads.append(pltpu.make_async_copy(lse_hbm, lse_s, in_ld.at[s]))
    for c in in_loads:
        c.start()

    bar = pltpu.get_barrier_semaphore()
    for dev in (up, up + 1, down, down + 1, partner):
        pl.semaphore_signal(bar, inc=1, device_id=(dev,), device_id_type=MESH)
    pl.semaphore_wait(bar, 5)

    def own_copy(u):
        m = u // 2
        src = kraw.at[4 + k, m] if u % 2 == 0 else kv_x.at[m]
        dev = up + par(u)
        return remote(src, kraw.at[2 + k, m], o_send.at[u], o_recv.at[k, m], dev)

    def own_arrival(u):
        m = u // 2
        x = par(u)
        return remote(kraw.at[2 + x, m], kraw.at[2 + x, m], o_send.at[u], o_recv.at[x, m], up)

    def relay_copy(u):
        m = u // 2
        x = par(u)
        return remote(kraw.at[2 + x, m], kraw.at[x, m], r_send.at[u], r_recv.at[x, m], up + k)

    def g2_copy(u):
        m = u // 2
        x = par(u)
        return remote(g2s.at[x, m], g2r.at[x, m], g2_send.at[u], g2_recv.at[x, m], down + k)

    def g1_copy(u):
        m = u // 2
        x = par(u)
        return remote(g1s.at[x, m], g1r.at[k, m], g1_send.at[u], g1_recv.at[k, m], down + x)

    def g1_arrival(u):
        m = u // 2
        p = par(u)
        return remote(g1s.at[p, m], g1r.at[p, m], g1_send.at[u], g1_recv.at[p, m], down)

    x_kv = remote(kv_x, kraw.at[4 + k], x_send.at[0], x_recv.at[0], partner)
    x_q = remote(qx, qb.at[k], x_send.at[1], x_recv.at[1], partner)
    x_g = remote(gx, gb.at[k], x_send.at[2], x_recv.at[2], partner)
    x_st = remote(stx, st.at[k], x_send.at[3], x_recv.at[3], partner)
    g0_copy = remote(acc_l.at[oth], g0r, x_send.at[4], x_recv.at[4], partner)

    def kv_wait(m, i):
        for e in range(2):
            kv_loads[(m * 2 + i) * 2 + e].wait()

    kv_wait(0, 0)
    own_copy(0).start()
    kv_wait(0, 1)
    own_copy(1).start()
    for m in range(1, NC):
        kv_wait(m, 0)
        kv_wait(m, 1)
    x_kv.start()
    for i in (2, 3):
        in_loads[i].wait()
    x_q.start()
    for i in (6, 7):
        in_loads[i].wait()
    x_g.start()
    for i in (0, 1, 4, 5, 8, 9, 10, 11, 12):
        in_loads[i].wait()

    def flat(val):
        return val.reshape(val.shape[0] * 2, HD)

    lse = lse_s[...] * LOG2E
    hi = lse.astype(BF)
    rest = lse - hi.astype(F32)
    mid = rest.astype(BF)
    low = (rest - mid.astype(F32)).astype(BF)
    parts = jnp.concatenate([hi.astype(F32), mid.astype(F32), low.astype(F32), jnp.zeros_like(lse)], 0).astype(BF)
    row = lax.broadcasted_iota(jnp.int32, (T, 2 * T), 0)
    col = lax.broadcasted_iota(jnp.int32, (T, 2 * T), 1)
    wide = []
    for e in range(2):
        place = jnp.where(col == 2 * row + e, 1.0, 0.0).astype(BF)
        r = dot_nn(parts, place)
        wide.append(r[0:8] + r[8:16] + r[16:24])
    lse_w = [wide[0][2 * i : 2 * i + 1] + wide[1][2 * i + 1 : 2 * i + 2] for i in range(4)]
    ones = jnp.ones((8, HD), BF)

    def delta_of(a, b):
        prod = a.astype(F32) * b.astype(F32)
        top = prod.astype(BF)
        left = (prod - top.astype(F32)).astype(BF)
        return (dot_nt(ones, top) + dot_nt(ones, left))[0:1]

    no_1 = jnp.where(chip < 1, FAR, 0.0).astype(F32)
    no_2 = jnp.where(chip < 2, FAR, 0.0).astype(F32)
    for j in range(2):
        for which in range(2):
            if which == 0:
                dst, dl = st.at[k, j], delta_of(flat(gb[k, j]), flat(ob[0, j]))
            else:
                dst, dl = stx.at[j], delta_of(flat(gx[j]), flat(ob[1, j]))
            if which == 0:
                lw = jnp.where(k == 0, lse_w[j], lse_w[2 + j])
            else:
                lw = jnp.where(k == 0, lse_w[2 + j], lse_w[j])
            dst[0:1, :] = lw
            dst[1:2, :] = dl
            dst[2:3, :] = lw + no_1
            dst[3:4, :] = lw + no_2
            dst[4:8, :] = jnp.zeros((4, 2 * T), F32)
    x_st.start()
    dq_t[...] = jnp.zeros_like(dq_t)

    def split(src, slot):
        for e in range(2):
            kf[slot, e] = flat(src[e]).astype(F32)
        for e in range(2):
            for j in range(2):
                kd[slot, e, j] = kf[slot, e, pl.ds(j, TC, stride=2), :].astype(BF)

    def tile(slot, b, j, lo, hi, norm_row, mask):
        kc, vc = kd[slot, 0, j], kd[slot, 1, j]
        q, g = flat(qb[b, j, lo // 2 : hi // 2]), flat(gb[b, j, lo // 2 : hi // 2])
        sc = dot_nt(kc, q)
        p = jnp.exp2(sc * (SCALE * LOG2E) - st[b, j, norm_row : norm_row + 1, lo:hi])
        if mask is not None:
            p = jnp.where(mask, p, 0.0)
        dv = dot_nn(p.astype(BF), g)
        dp = dot_nt(vc, g)
        ds = (p * (dp - st[b, j, 1:2, lo:hi])).astype(BF)
        dk = dot_nn(ds, q)
        dq_t[b, j, :, lo:hi] += dot_tn(kc, ds)
        return dk, dv

    def tri(m, lo, hi, upper):
        key = m * TC + lax.broadcasted_iota(jnp.int32, (TC, hi - lo), 0)
        tok = (lo + lax.broadcasted_iota(jnp.int32, (TC, hi - lo), 1)) // 2
        return key > tok if upper else tok >= key

    def local_causal(x):
        for m in range(NC):
            split(kraw.at[4 + x, m], 0)
            lo = 2 * m * TC
            for j in range(2):
                dk, dv = tile(0, x, j, lo, 2 * T, 0, tri(m, lo, 2 * T, False))
                acc_l[x, 0, j, pl.ds(m * TC, TC), :] = dk
                acc_l[x, 1, j, pl.ds(m * TC, TC), :] = dv

    def local_full():
        for m in range(NC):
            split(kraw.at[4, m], 0)
            for j in range(2):
                dk, dv = tile(0, 1, j, 0, 2 * T, 0, None)
                acc_l[0, 0, j, pl.ds(m * TC, TC), :] += dk
                acc_l[0, 1, j, pl.ds(m * TC, TC), :] += dv

    def near_unit(u):
        m, x = u // 2, par(u)
        split(kraw.at[2 + x, m], 1)
        for j in range(2):
            dk0, dv0 = tile(1, 0, j, 0, 2 * T, 2, None)
            dk1, dv1 = tile(1, 1, j, 0, 2 * T, 2, None)
            acc_h[x, m, 0, j] = dk0 + dk1
            acc_h[x, m, 1, j] = dv0 + dv1

    def far_unit(u):
        m, x = u // 2, par(u)
        split(kraw.at[x, m], 2)
        hi = 2 * (m + 1) * TC
        for j in range(2):
            dk, dv = tile(2, x, j, 0, hi, 3, tri(m, 0, hi, True))
            acc_z[0, j] = dk
            acc_z[1, j] = dv

        @pl.when(x == 1)
        def _():
            for j in range(2):
                dk, dv = tile(2, 0, j, 0, 2 * T, 3, None)
                acc_z[0, j] += dk
                acc_z[1, j] += dv

        g2s[x, m] = acc_z[...].astype(BF)

    def near_finish(u):
        m, x = u // 2, par(u)
        g1s[x, m] = (acc_h[x, m] + g2r[x, m].astype(F32)).astype(BF)

    outs = []

    def final_unit(u):
        m, p = u // 2, par(u)
        rows = pl.ds(m * TC, TC)
        for e in range(2):
            for j in range(2):
                mine = acc_l[k, e, j, rows, :] if u % 2 == 0 else g0r[e, j, rows, :]
                val = mine + g1r[p, m, e, j].astype(F32)
                if e == 0:
                    val = val * SCALE
                fi[e, pl.ds(j, TC, stride=2), :] = val
            fo[u, e] = fi[e].astype(BF).reshape(TC, 2, HD)
            dst = (gk_out, gv_out)[e]
            c = pltpu.make_async_copy(fo.at[u, e], dst.at[rows, p], out_sem.at[2 * u + e])
            c.start()
            outs.append(c)

    def arrive(u):
        own_arrival(u).wait_recv()
        relay_copy(u).start()
        if u + 2 < NU:
            own_copy(u + 2).start()

    def far_step(u):
        relay_copy(u).wait_recv()
        far_unit(u)
        g2_copy(u).start()

    def near_step(u):
        g2_copy(u).wait_recv()
        near_finish(u)
        g1_copy(u).start()

    def final_step(u):
        g1_arrival(u).wait_recv()
        final_unit(u)

    local_causal(k)
    arrive(0)
    x_kv.wait_recv()
    x_q.wait_recv()
    x_g.wait_recv()
    x_st.wait_recv()
    local_causal(oth)
    arrive(1)
    local_full()
    g0_copy.start()
    near_unit(0)
    near_unit(1)
    far_step(0)
    for u in range(2, NU):
        arrive(u)
        near_unit(u)
        far_step(u - 1)
        near_step(u - 2)
        if u == 4:
            g0_copy.wait_recv()
        if u >= 4:
            final_step(u - 4)
    far_step(NU - 1)

    dq_copies = []
    for j in range(2):
        for b, dst_dev in ((oth, partner), (k, None)):
            dqs[b, j] = (dq_t[b, j].T * SCALE).astype(BF).reshape(T, 2, HD)
            if dst_dev is None:
                c = pltpu.make_async_copy(dqs.at[b, j], gq_out.at[:, 2 * k + j], out_sem.at[2 * NU + j])
                c.start()
                outs.append(c)
            else:
                c = remote(dqs.at[b, j], gq_out.at[:, 2 * k + j], dq_send.at[j], dq_recv.at[j], partner)
                c.start()
                dq_copies.append(c)

    near_step(NU - 2)
    final_step(NU - 4)
    final_step(NU - 3)
    near_step(NU - 1)
    final_step(NU - 2)
    final_step(NU - 1)

    for u in range(NU):
        own_copy(u).wait_send()
        relay_copy(u).wait_send()
        g2_copy(u).wait_send()
        g1_copy(u).wait_send()
    for c in (x_kv, x_q, x_g, x_st, g0_copy):
        c.wait_send()
    for c in dq_copies:
        c.wait()
    for c in outs:
        c.wait()


def shards(n, queries, key_rows, value_rows, attn_output, grad_output, log_norm):
    heads4 = (T, 4, 2, HD)
    heads2 = (T, 2, 2, HD)
    anym = pl.BlockSpec(memory_space=pl.ANY)
    dma = pltpu.SemaphoreType.DMA
    vm = pltpu.VMEM
    pair = (T, 2, HD)
    scratch = [
        vm((6, NC, 2, TC, 2, HD), BF),
        vm((NC, 2, TC, 2, HD), BF),
        vm((2, 2) + pair, BF),
        vm((2, 2) + pair, BF),
        vm((2,) + pair, BF),
        vm((2,) + pair, BF),
        vm((2, 2) + pair, BF),
        vm((8, T), F32),
        vm((2, 2, 8, 2 * T), F32),
        vm((2, 8, 2 * T), F32),
        vm((3, 2, 2, TC, HD), BF),
        vm((3, 2, 2 * TC, HD), F32),
        vm((2, NC, 2, 2, TC, HD), F32),
        vm((2, 2, 2, T, HD), F32),
        vm((2, 2, TC, HD), F32),
        vm((2, 2, HD, 2 * T), F32),
        vm((2, 2) + pair, BF),
        vm((2, NC, 2, 2, TC, HD), BF),
        vm((2, NC, 2, 2, TC, HD), BF),
        vm((2, NC, 2, 2, TC, HD), BF),
        vm((2, NC, 2, 2, TC, HD), BF),
        vm((2, 2, T, HD), F32),
        vm((2, 2 * TC, HD), F32),
        vm((NU, 2, TC, 2, HD), BF),
        dma((NC, 2, 2)),
        dma((13,)),
        dma((NU,)), dma((2, NC)),
        dma((NU,)), dma((2, NC)),
        dma((NU,)), dma((2, NC)),
        dma((NU,)), dma((2, NC)),
        dma((5,)), dma((5,)),
        dma((2,)), dma((2,)),
        dma((2 * NU + 2,)),
    ]
    gq, gk, gv = pl.pallas_call(
        functools.partial(kernel, n),
        out_shape=(
            jax.ShapeDtypeStruct(heads4, BF),
            jax.ShapeDtypeStruct(heads2, BF),
            jax.ShapeDtypeStruct(heads2, BF),
        ),
        in_specs=[anym] * 6,
        out_specs=(anym,) * 3,
        scratch_shapes=scratch,
        compiler_params=pltpu.CompilerParams(
            collective_id=0, has_side_effects=True, vmem_limit_bytes=48 << 20
        ),
    )(
        queries.reshape(heads4),
        key_rows.reshape(heads2),
        value_rows.reshape(heads2),
        attn_output.reshape(heads4),
        grad_output.reshape(heads4),
        log_norm,
    )
    return (
        gq.reshape(queries.shape),
        gk.reshape(key_rows.shape),
        gv.reshape(value_rows.shape),
    )


def solution(mesh):
    wide = P("seq", None, None)
    return jax.shard_map(
        functools.partial(shards, mesh.shape["seq"]),
        mesh=mesh,
        in_specs=(wide, wide, wide, wide, wide, P(None, "seq")),
        out_specs=(wide, wide, wide),
        check_vma=False,
    )
```

time: 98.9 us -> 70.1 us (0.71)
  the two profiles are of different devices: /device:TPU:6 before, /device:TPU:1 now
where the time goes in v1:
time: 70.1 us; the launch traced here: 69.7 us
  Pallas kernels  61.2 us (87%)
  local copies, waits for them, and re-layouts  7.91 us (11%)
    pallas_call x1, Pallas kernels, shards(): pl.pallas_call(functools.partial(kernel, n), out_shape=(jax.ShapeDtypeStr...  61.2 us
    unnamed x15, local copies, waits for them, and re-layouts  7.91 us

profile of v1, /device:TPU:1, one launch (start us, length us, event | category | flops | bytes accessed | tf_op | source)
XLA Modules:
  0.0 69.7 jit_solution(15857309211911187620)
XLA Ops:
  0.6 0.0 copy-start.5
  0.6 0.7 copy-done.5
  1.3 0.0 copy-start
  1.3 1.0 %copy-done = bf16[256,8,128]{2,1,0:T(8,128)(2,1)S(1)} copy-done((bf16[256,8,128]{2,1,0:T(8,128)(2,1)S(1)}, bf16[256,8,128]{2,1,0:T(8,128)(2,1)}, u32[]{:S(2)}) %copy-start) | copy-done | bytes 524312
  2.4 0.0 copy-start.1
  2.4 1.0 %copy-done.1 = bf16[256,8,128]{2,1,0:T(8,128)(2,1)S(1)} copy-done((bf16[256,8,128]{2,1,0:T(8,128)(2,1)S(1)}, bf16[256,8,128]{2,1,0:T(8,128)(2,1)}, u32[]{:S(2)}) %copy-start.1) | copy-done | bytes 524312
  3.4 0.0 copy-start.2
  3.4 1.0 %copy-done.2 = bf16[256,8,128]{2,1,0:T(8,128)(2,1)S(1)} copy-done((bf16[256,8,128]{2,1,0:T(8,128)(2,1)S(1)}, bf16[256,8,128]{2,1,0:T(8,128)(2,1)}, u32[]{:S(2)}) %copy-start.2) | copy-done | bytes 524312
  4.5 0.0 copy-start.3
  4.5 0.9 %copy-done.3 = bf16[256,4,128]{2,1,0:T(4,128)(2,1)S(1)} copy-done((bf16[256,4,128]{2,1,0:T(4,128)(2,1)S(1)}, bf16[256,4,128]{2,1,0:T(4,128)(2,1)}, u32[]{:S(2)}) %copy-start.3) | copy-done | bytes 262168
  5.4 0.0 copy-start.4
  5.4 0.9 %copy-done.4 = bf16[256,4,128]{2,1,0:T(4,128)(2,1)S(1)} copy-done((bf16[256,4,128]{2,1,0:T(4,128)(2,1)S(1)}, bf16[256,4,128]{2,1,0:T(4,128)(2,1)}, u32[]{:S(2)}) %copy-start.4) | copy-done | bytes 262168
  6.4 61.2 %shard_map.85 = (bf16[256,4,2,128]{3,2,1,0:T(2,128)(2,1)S(1)}, bf16[256,2,2,128]{3,2,1,0:T(2,128)(2,1)S(1)}, bf16[256,2,2,128]{3,2,1,0:T(2,128)(2,1)S(1)}) custom-call(bf16[256,4,2,128]{3,2,1,0:T(2,128)(2,1)S(1)} %bitcast.9, bf16[256,2,2,128]{3,2,1,0:T(2,128)(2,1)S(1)} %bitcast.14, bf16[256,2,2,128]{3,2,1,0:T(2,128)(2,1)S(1)} %bitcast.15, ...), custom_call_target="tpu_custom_call" | custom-call | tf_op jit(solution)/shard_map/pallas_call | solution.py:405
  67.5 0.8 %copy.12 = bf16[256,8,128]{2,1,0:T(8,128)(2,1)} copy(bf16[256,8,128]{2,1,0:T(8,128)(2,1)S(1)} %bitcast.8) | data formatting | bytes 1048576
  68.3 0.7 %copy.13 = bf16[256,4,128]{2,1,0:T(4,128)(2,1)} copy(bf16[256,4,128]{2,1,0:T(4,128)(2,1)S(1)} %bitcast.13) | data formatting | bytes 524288
  69.0 0.7 %copy.14 = bf16[256,4,128]{2,1,0:T(4,128)(2,1)} copy(bf16[256,4,128]{2,1,0:T(4,128)(2,1)S(1)} %bitcast.12) | data formatting | bytes 524288
Async XLA Ops:
  0.6 0.7 %copy-start.5 = (f32[8,256]{1,0:T(8,128)S(1)}, f32[8,256]{1,0:T(8,128)}, u32[]{:S(2)}) copy-start(f32[8,256]{1,0:T(8,128)} %lse_hbm.1) | copy-start | bytes 24580
  1.3 1.0 %copy-start = (bf16[256,8,128]{2,1,0:T(8,128)(2,1)S(1)}, bf16[256,8,128]{2,1,0:T(8,128)(2,1)}, u32[]{:S(2)}) copy-start(bf16[256,8,128]{2,1,0:T(8,128)(2,1)} %param.6) | copy-start | bytes 1572868
  2.4 1.0 %copy-start.1 = (bf16[256,8,128]{2,1,0:T(8,128)(2,1)S(1)}, bf16[256,8,128]{2,1,0:T(8,128)(2,1)}, u32[]{:S(2)}) copy-start(bf16[256,8,128]{2,1,0:T(8,128)(2,1)} %param.9) | copy-start | bytes 1572868
  3.4 1.0 %copy-start.2 = (bf16[256,8,128]{2,1,0:T(8,128)(2,1)S(1)}, bf16[256,8,128]{2,1,0:T(8,128)(2,1)}, u32[]{:S(2)}) copy-start(bf16[256,8,128]{2,1,0:T(8,128)(2,1)} %param.10) | copy-start | bytes 1572868
  4.5 0.9 %copy-start.3 = (bf16[256,4,128]{2,1,0:T(4,128)(2,1)S(1)}, bf16[256,4,128]{2,1,0:T(4,128)(2,1)}, u32[]{:S(2)}) copy-start(bf16[256,4,128]{2,1,0:T(4,128)(2,1)} %param.7) | copy-start | bytes 786436
  5.4 0.9 %copy-start.4 = (bf16[256,4,128]{2,1,0:T(4,128)(2,1)S(1)}, bf16[256,4,128]{2,1,0:T(4,128)(2,1)}, u32[]{:S(2)}) copy-start(bf16[256,4,128]{2,1,0:T(4,128)(2,1)} %param.8) | copy-start | bytes 786436

commit v2 on v1

v2 whole, which is shorter than its diff:
```python
import functools
import math

import jax
import jax.numpy as jnp
from jax import lax
from jax.experimental import pallas as pl
from jax.experimental.pallas import tpu as pltpu
from jax.sharding import PartitionSpec as P

MESH = pl.DeviceIdType.MESH
BF = jnp.bfloat16
F32 = jnp.float32
SCALE = 168.0 ** (-0.5)
LOG2E = math.log2(math.e)
T = 256
HD = 128
NC = 4
TC = T // NC
NU = 2 * NC
FAR = 1e30
VMEM_KIB = 24 << 10
DIRECT_KV = ()
DIRECT_G = (3,)
PLAN = ('flip0', 'A0', 'A1', 'o2', 'X', 'flip1', 'L0', 'N0', 'F0', 'A2', 'A3', 'o3', 'N1', 'L1', 'S0', 'F1', 'A4', 'A5', 'LF', 'S1', 'F2', 'A6', 'A7', 'N2', 'N3', 'S3', 'F3', 'S2', 'Q', 'Z0', 'Z1', 'Z2', 'Z3', 'D', 'Z4', 'Z5', 'Z6', 'Z7')


def dot_nt(a, b):
    return lax.dot_general(a, b, (((1,), (1,)), ((), ())), preferred_element_type=F32)


def dot_nn(a, b):
    return lax.dot_general(a, b, (((1,), (0,)), ((), ())), preferred_element_type=F32)


def dot_tn(a, b):
    return lax.dot_general(a, b, (((0,), (0,)), ((), ())), preferred_element_type=F32)


def kernel(
    n,
    q_hbm, k_hbm, v_hbm, o_hbm, g_hbm, lse_hbm,
    gq_out, gk_out, gv_out,
    kin, kraw, kv_x, qraw, graw, ob, qf, gf, qt, gt, qx, gx, lse_s, st, stx, kf,
    acc_h, acc_l, dq_t, dqs, g2s, g2r, g1s, g1r, g2d, g0r, fi, fo,
    kv_ld, in_ld,
    o_send, o_recv, r_send, r_recv, g2_send, g2_recv, g1_send, g1_recv, gd_send, gd_recv,
    x_send, x_recv, dq_send, dq_recv, out_sem,
):
    me = lax.axis_index("seq")
    k = lax.rem(me, 2)
    oth = 1 - k
    chip = lax.div(me, 2)
    up = lax.rem(me - k + 2, n)
    down = lax.rem(me - k + n - 2, n)
    up2 = lax.rem(me - k + 4, n)
    down2 = lax.rem(me - k + n - 4, n)
    partner = me - k + oth

    def remote(src, dst, ssem, rsem, dev):
        return pltpu.make_async_remote_copy(
            src_ref=src, dst_ref=dst, send_sem=ssem, recv_sem=rsem,
            device_id=(dev,), device_id_type=MESH,
        )

    def par(u):
        return k if u % 2 == 0 else oth

    kv_loads = []
    for m in range(NC):
        rows = pl.ds(m * TC, TC)
        for i, pair in enumerate((k, oth)):
            for e, src in enumerate((k_hbm, v_hbm)):
                kv_loads.append(
                    pltpu.make_async_copy(src.at[rows, pair], kin.at[i, m, e], kv_ld.at[m, i, e])
                )
    for c in kv_loads:
        c.start()
    in_loads = []
    s = 0
    for src, dst2 in ((q_hbm, qraw), (g_hbm, graw), (o_hbm, ob)):
        for i, base in enumerate((k, oth)):
            for j in range(2):
                in_loads.append(
                    pltpu.make_async_copy(src.at[:, 2 * base + j], dst2.at[i, j], in_ld.at[s])
                )
                s += 1
    in_loads.append(pltpu.make_async_copy(lse_hbm, lse_s, in_ld.at[s]))
    for c in in_loads:
        c.start()

    bar = pltpu.get_barrier_semaphore()
    for dev in (up, up + 1, down, down + 1, up2, up2 + 1, down2, down2 + 1, partner):
        pl.semaphore_signal(bar, inc=1, device_id=(dev,), device_id_type=MESH)
    pl.semaphore_wait(bar, 9)

    def own_copy(u):
        m = u // 2
        src = kraw.at[4 + k, m] if u % 2 == 0 else kv_x.at[m]
        dev = up + par(u)
        return remote(src, kraw.at[2 + k, m], o_send.at[u], o_recv.at[k, m], dev)

    def own_arrival(u):
        m = u // 2
        x = par(u)
        return remote(kraw.at[2 + x, m], kraw.at[2 + x, m], o_send.at[u], o_recv.at[x, m], up)

    def direct_copy(u):
        m = u // 2
        src = kraw.at[4 + k, m] if u % 2 == 0 else kv_x.at[m]
        return remote(src, kraw.at[k, m], r_send.at[u], r_recv.at[k, m], up2 + par(u))

    def relay_copy(u):
        m = u // 2
        x = par(u)
        return remote(kraw.at[2 + x, m], kraw.at[x, m], r_send.at[u], r_recv.at[x, m], up + k)

    def g2_copy(m, j):
        return remote(g2s.at[m, j], g2r.at[m, j], g2_send.at[m, j], g2_recv.at[m, j], down + k)

    def g2d_copy(u):
        m, x = u // 2, par(u)
        return remote(g2s.at[m, :, x], g2d.at[k, m], gd_send.at[u], gd_recv.at[k, m], down2 + x)

    def g2d_arrival(u):
        m, p = u // 2, par(u)
        return remote(g2s.at[m, :, p], g2d.at[p, m], gd_send.at[u], gd_recv.at[p, m], down2)

    def g1_copy(u):
        m = u // 2
        x = par(u)
        return remote(g1s.at[m, x], g1r.at[k, m], g1_send.at[u], g1_recv.at[k, m], down + x)

    def g1_arrival(u):
        m = u // 2
        p = par(u)
        return remote(g1s.at[m, p], g1r.at[p, m], g1_send.at[u], g1_recv.at[p, m], down)

    x_kv = remote(kv_x, kraw.at[4 + k], x_send.at[0], x_recv.at[0], partner)
    x_q = remote(qx, qf.at[k], x_send.at[1], x_recv.at[1], partner)
    x_g = remote(gx, gf.at[k], x_send.at[2], x_recv.at[2], partner)
    x_st = remote(stx, st.at[k], x_send.at[3], x_recv.at[3], partner)
    g0_copy = remote(acc_l.at[oth], g0r, x_send.at[4], x_recv.at[4], partner)

    def kv_wait(m, i):
        for e in range(2):
            kv_loads[(m * 2 + i) * 2 + e].wait()

    def flat(val):
        return val.reshape(val.shape[0] * 2, HD)

    def split(m):
        for i, dst in enumerate((kraw.at[4 + k, m], kv_x.at[m])):
            kv_wait(m, i)
            for e in range(2):
                kf[e] = flat(kin[i, m, e]).astype(F32)
                for j in range(2):
                    dst[e, j] = kf[e, pl.ds(j, TC, stride=2), :].astype(BF)

    for m in range(NC):
        split(m)
        if m < 2:
            own_copy(2 * m).start()
            own_copy(2 * m + 1).start()
    x_kv.start()
    for raw, near, far, first, copy in ((qraw, qf, qx, 0, x_q), (graw, gf, gx, 4, x_g)):
        for j in range(2):
            in_loads[first + 2 + j].wait()
            far[j] = flat(raw[1, j])
        copy.start()
        for j in range(2):
            in_loads[first + j].wait()
            near[k, j] = flat(raw[0, j])
    for i in range(8, 13):
        in_loads[i].wait()

    lse = lse_s[...] * LOG2E
    hi = lse.astype(BF)
    rest = lse - hi.astype(F32)
    mid = rest.astype(BF)
    low = (rest - mid.astype(F32)).astype(BF)
    parts = jnp.concatenate([hi.astype(F32), mid.astype(F32), low.astype(F32), jnp.zeros_like(lse)], 0).astype(BF)
    row = lax.broadcasted_iota(jnp.int32, (T, 2 * T), 0)
    col = lax.broadcasted_iota(jnp.int32, (T, 2 * T), 1)
    wide = []
    for e in range(2):
        place = jnp.where(col == 2 * row + e, 1.0, 0.0).astype(BF)
        r = dot_nn(parts, place)
        wide.append(r[0:8] + r[8:16] + r[16:24])
    lse_w = [wide[0][2 * i : 2 * i + 1] + wide[1][2 * i + 1 : 2 * i + 2] for i in range(4)]
    ones = jnp.ones((8, HD), BF)

    def delta_of(a, b):
        prod = a.astype(F32) * b.astype(F32)
        top = prod.astype(BF)
        left = (prod - top.astype(F32)).astype(BF)
        return (dot_nt(ones, top) + dot_nt(ones, left))[0:1]

    no_1 = jnp.where(chip < 1, FAR, 0.0).astype(F32)
    no_2 = jnp.where(chip < 2, FAR, 0.0).astype(F32)
    for j in range(2):
        for which in range(2):
            if which == 0:
                dst, dl = st.at[k, j], delta_of(gf[k, j], flat(ob[0, j]))
            else:
                dst, dl = stx.at[j], delta_of(gx[j], flat(ob[1, j]))
            if which == 0:
                lw = jnp.where(k == 0, lse_w[j], lse_w[2 + j])
            else:
                lw = jnp.where(k == 0, lse_w[2 + j], lse_w[j])
            dst[0:1, :] = lw
            dst[1:2, :] = dl
            dst[2:3, :] = lw + no_1
            dst[3:4, :] = lw + no_2
            dst[4:8, :] = jnp.zeros((4, 2 * T), F32)
    x_st.start()
    dq_t[...] = jnp.zeros_like(dq_t)

    def flip(b):
        for j in range(2):
            qt[b, j] = qf[b, j].T
            gt[b, j] = gf[b, j].T

    def tile(kc, vc, b, j, lo, norm_row, mask):
        q, g = qf[b, j, lo:, :], gf[b, j, lo:, :]
        sc = dot_nn(kc, qt[b, j, :, lo:])
        dp = dot_nn(vc, gt[b, j, :, lo:])
        p = jnp.exp2(sc * (SCALE * LOG2E) - st[b, j, norm_row : norm_row + 1, lo:])
        if mask is not None:
            p = jnp.where(mask, p, 0.0)
        dv = dot_nn(p.astype(BF), g)
        ds = (p * (dp - st[b, j, 1:2, lo:])).astype(BF)
        dk = dot_nn(ds, q)
        dq_t[b, j, :, lo:] += dot_tn(kc, ds)
        return dk, dv

    def keys(j, *parts):
        return [jnp.concatenate([kraw[x, m, e, j] for x, m in parts], 0) for e in range(2)]

    def heads(body):
        lax.fori_loop(0, 2, lambda j, c: (body(j), c)[1], 0)

    def grid2(rows, lo):
        row = lax.broadcasted_iota(jnp.int32, (rows, 2 * T - lo), 0)
        tok = (lo + lax.broadcasted_iota(jnp.int32, (rows, 2 * T - lo), 1)) // 2
        return row, tok

    R = 2 * TC

    def local_causal(x):
        for h in range(NC // 2):
            lo = 2 * h * R

            def body(j):
                row, tok = grid2(R, lo)
                kc, vc = keys(j, (4 + x, 2 * h), (4 + x, 2 * h + 1))
                dk, dv = tile(kc, vc, x, j, lo, 0, tok >= row + h * R)
                acc_l[x, 0, j, pl.ds(h * R, R), :] = dk
                acc_l[x, 1, j, pl.ds(h * R, R), :] = dv

            heads(body)

    def local_full():
        for h in range(NC // 2):

            def body(j):
                kc, vc = keys(j, (4, 2 * h), (4, 2 * h + 1))
                dk, dv = tile(kc, vc, 1, j, 0, 0, None)
                acc_l[0, 0, j, pl.ds(h * R, R), :] += dk
                acc_l[0, 1, j, pl.ds(h * R, R), :] += dv

            heads(body)

    def near(m):
        def body(j):
            kc, vc = keys(j, (2, m), (3, m))
            dk0, dv0 = tile(kc, vc, 0, j, 0, 2, None)
            dk1, dv1 = tile(kc, vc, 1, j, 0, 2, None)
            acc_h[m, 0, j] = dk0 + dk1
            acc_h[m, 1, j] = dv0 + dv1

        heads(body)

    def far(m):
        def body(j):
            row, tok = grid2(R, 0)
            kc, vc = keys(j, (0, m), (1, m))
            dk0, dv0 = tile(kc, vc, 0, j, 0, 3, (row >= TC) | (row + m * TC > tok))
            row, tok = grid2(TC, 0)
            dk1, dv1 = tile(kc[TC:], vc[TC:], 1, j, 0, 3, row + m * TC > tok)
            g2s[m, j, 0, 0] = dk0[:TC].astype(BF)
            g2s[m, j, 0, 1] = dv0[:TC].astype(BF)
            g2s[m, j, 1, 0] = (dk0[TC:] + dk1).astype(BF)
            g2s[m, j, 1, 1] = (dv0[TC:] + dv1).astype(BF)
            if m not in DIRECT_G:
                g2_copy(m, j).start()

        heads(body)

    def near_finish(m):
        for j in range(2):
            if m not in DIRECT_G:
                g2_copy(m, j).wait_recv()
            for x in range(2):
                for e in range(2):
                    val = acc_h[m, e, j, x * TC : (x + 1) * TC]
                    if m not in DIRECT_G:
                        val = val + g2r[m, j, x, e].astype(F32)
                    g1s[m, x, e, j] = val.astype(BF)

    outs = []

    def final_unit(u):
        m, p = u // 2, par(u)
        rows = pl.ds(m * TC, TC)
        for e in range(2):
            for j in range(2):
                mine = acc_l[k, e, j, rows, :] if u % 2 == 0 else g0r[e, j, rows, :]
                val = mine + g1r[p, m, e, j].astype(F32)
                if m in DIRECT_G:
                    val = val + g2d[p, m, j, e].astype(F32)
                if e == 0:
                    val = val * SCALE
                fi[e, pl.ds(j, TC, stride=2), :] = val
            fo[u, e] = fi[e].astype(BF)
            dst = (gk_out, gv_out)[e]
            c = pltpu.make_async_copy(fo.at[u, e], dst.at[p, pl.ds(2 * m * TC, 2 * TC)], out_sem.at[2 * u + e])
            c.start()
            outs.append(c)

    def arrive(u):
        own_arrival(u).wait_recv()
        if u // 2 not in DIRECT_KV:
            relay_copy(u).start()

    def own_send(m):
        own_copy(2 * m).start()
        own_copy(2 * m + 1).start()

    def far_step(m):
        relay_copy(2 * m).wait_recv()
        relay_copy(2 * m + 1).wait_recv()
        far(m)
        if m in DIRECT_G:
            g2d_copy(2 * m).start()
            g2d_copy(2 * m + 1).start()

    def near_step(m):
        near_finish(m)
        g1_copy(2 * m).start()
        g1_copy(2 * m + 1).start()

    def final_step(u):
        g1_arrival(u).wait_recv()
        if u // 2 in DIRECT_G:
            g2d_arrival(u).wait_recv()
        final_unit(u)

    def from_partner():
        for c in (x_kv, x_q, x_g, x_st):
            c.wait_recv()

    def local_rest():
        local_full()
        g0_copy.start()

    dq_copies = []

    def query_grads():
        for j in range(2):
            for b in (oth, k):
                dqs[b, j] = (dq_t[b, j].T * SCALE).astype(BF)
            c = remote(dqs.at[oth, j], gq_out.at[2 * k + j], dq_send.at[j], dq_recv.at[j], partner)
            c.start()
            dq_copies.append(c)
            c = pltpu.make_async_copy(dqs.at[k, j], gq_out.at[2 * k + j], out_sem.at[2 * NU + j])
            c.start()
            outs.append(c)

    steps = {
        "flip0": lambda: flip(k), "flip1": lambda: flip(oth),
        "L0": lambda: local_causal(k), "L1": lambda: local_causal(oth), "LF": local_rest,
        "X": from_partner, "Q": lambda: g0_copy.wait_recv(), "D": query_grads,
    }
    by_index = {"A": arrive, "o": own_send, "N": near, "F": far_step, "S": near_step, "Z": final_step}
    for word in PLAN:
        if word in steps:
            steps[word]()
        else:
            by_index[word[0]](int(word[1:]))

    for u in range(NU):
        own_copy(u).wait_send()
        (direct_copy if u // 2 in DIRECT_KV else relay_copy)(u).wait_send()
        g1_copy(u).wait_send()
        if u // 2 in DIRECT_G:
            g2d_copy(u).wait_send()
    for m in range(NC):
        if m not in DIRECT_G:
            for j in range(2):
                g2_copy(m, j).wait_send()
    for c in (x_kv, x_q, x_g, x_st, g0_copy):
        c.wait_send()
    for c in dq_copies:
        c.wait()
    for c in outs:
        c.wait()


def deliver(q_in, k_in, v_in, q_out, k_out, v_out, sem):
    copies = []
    for src, dst in ((q_in, q_out), (k_in, k_out), (v_in, v_out)):
        for p in range(src.shape[0]):
            copies.append(pltpu.make_async_copy(src.at[p], dst.at[:, p], sem.at[len(copies)]))
    for c in copies:
        c.start()
    for c in copies:
        c.wait()


def shards(n, queries, key_rows, value_rows, attn_output, grad_output, log_norm):
    heads4 = (T, 4, 2, HD)
    heads2 = (T, 2, 2, HD)
    anym = pl.BlockSpec(memory_space=pl.ANY)
    dma = pltpu.SemaphoreType.DMA
    vm = pltpu.VMEM
    pair = (T, 2, HD)
    scratch = [
        vm((2, NC, 2, TC, 2, HD), BF),
        vm((6, NC, 2, 2, TC, HD), BF),
        vm((NC, 2, 2, TC, HD), BF),
        vm((2, 2) + pair, BF),
        vm((2, 2) + pair, BF),
        vm((2, 2) + pair, BF),
        vm((2, 2, 2 * T, HD), BF),
        vm((2, 2, 2 * T, HD), BF),
        vm((2, 2, HD, 2 * T), BF),
        vm((2, 2, HD, 2 * T), BF),
        vm((2, 2 * T, HD), BF),
        vm((2, 2 * T, HD), BF),
        vm((8, T), F32),
        vm((2, 2, 8, 2 * T), F32),
        vm((2, 8, 2 * T), F32),
        vm((2, 2 * TC, HD), F32),
        vm((NC, 2, 2, 2 * TC, HD), F32),
        vm((2, 2, 2, T, HD), F32),
        vm((2, 2, HD, 2 * T), F32),
        vm((2, 2, 2 * T, HD), BF),
        vm((NC, 2, 2, 2, TC, HD), BF),
        vm((NC, 2, 2, 2, TC, HD), BF),
        vm((NC, 2, 2, 2, TC, HD), BF),
        vm((2, NC, 2, 2, TC, HD), BF),
        vm((2, NC, 2, 2, TC, HD), BF),
        vm((2, 2, T, HD), F32),
        vm((2, 2 * TC, HD), F32),
        vm((NU, 2, 2 * TC, HD), BF),
        dma((NC, 2, 2)),
        dma((13,)),
        dma((NU,)), dma((2, NC)),
        dma((NU,)), dma((2, NC)),
        dma((NC, 2)), dma((NC, 2)),
        dma((NU,)), dma((2, NC)),
        dma((NU,)), dma((2, NC)),
        dma((5,)), dma((5,)),
        dma((2,)), dma((2,)),
        dma((2 * NU + 2,)),
    ]
    gq, gk, gv = pl.pallas_call(
        functools.partial(kernel, n),
        out_shape=(
            jax.ShapeDtypeStruct((4, 2 * T, HD), BF),
            jax.ShapeDtypeStruct((2, 2 * T, HD), BF),
            jax.ShapeDtypeStruct((2, 2 * T, HD), BF),
        ),
        in_specs=[pl.BlockSpec(memory_space=pltpu.HBM)] * 6,
        out_specs=(anym,) * 3,
        scratch_shapes=scratch,
        compiler_params=pltpu.CompilerParams(
            collective_id=0, has_side_effects=True, vmem_limit_bytes=VMEM_KIB << 10
        ),
    )(
        *(
            pltpu.with_memory_space_constraint(a, pltpu.HBM)
            for a in (
                queries.reshape(heads4),
                key_rows.reshape(heads2),
                value_rows.reshape(heads2),
                attn_output.reshape(heads4),
                grad_output.reshape(heads4),
                log_norm,
            )
        )
    )
    gq, gk, gv = pl.pallas_call(
        deliver,
        out_shape=tuple(jax.ShapeDtypeStruct(shape, BF) for shape in (heads4, heads2, heads2)),
        in_specs=[anym] * 3,
        out_specs=(pl.BlockSpec(memory_space=pltpu.HBM),) * 3,
        scratch_shapes=[dma((8,))],
        compiler_params=pltpu.CompilerParams(vmem_limit_bytes=1 << 20),
    )(*(a.reshape((a.shape[0],) + pair) for a in (gq, gk, gv)))
    return (
        gq.reshape(queries.shape),
        gk.reshape(key_rows.shape),
        gv.reshape(value_rows.shape),
    )


def solution(mesh):
    wide = P("seq", None, None)
    return jax.shard_map(
        functools.partial(shards, mesh.shape["seq"]),
        mesh=mesh,
        in_specs=(wide, wide, wide, wide, wide, P(None, "seq")),
        out_specs=(wide, wide, wide),
        check_vma=False,
    )
```

time: 70.1 us -> 52.3 us (0.75)
  Pallas kernels: 61.2 us -> 51.5 us
  local copies, waits for them, and re-layouts: 7.91 us -> 0 us
    pallas_call x1, Pallas kernels: 61.2 us -> 50.5 us  [shards(): pl.pallas_call(functools.partial(kernel, n), out_shape=(jax.ShapeDtypeStr...]
    unnamed x15 -> x0, local copies, waits for them, and re-layouts: 7.91 us -> none
    pallas_call x0 -> x1, Pallas kernels: none -> 1.03 us  [shards(): pl.pallas_call(deliver, out_shape=tuple((jax.ShapeDtypeStruct(shape, BF)...]
where the time goes in v2:
time: 52.3 us; the launch traced here: 52.2 us
  Pallas kernels  51.5 us (98%)
  between operations  0.64 us (1%)
    pallas_call x1, Pallas kernels, shards(): pl.pallas_call(functools.partial(kernel, n), out_shape=(jax.ShapeDtypeStr...  50.5 us

profile of v2, /device:TPU:1, one launch (start us, length us, event | category | flops | bytes accessed | tf_op | source)
XLA Modules:
  0.0 52.2 jit_solution(6226712458745931480)
XLA Ops:
  0.6 50.5 %shard_map.85 = (bf16[4,512,128]{2,1,0:T(8,128)(2,1)S(1)}, bf16[2,512,128]{2,1,0:T(8,128)(2,1)S(1)}, bf16[2,512,128]{2,1,0:T(8,128)(2,1)S(1)}) custom-call(bf16[256,4,2,128]{3,2,1,0:T(2,128)(2,1)} %bitcast.14, bf16[256,2,2,128]{3,2,1,0:T(2,128)(2,1)} %bitcast.17, bf16[256,2,2,128]{3,2,1,0:T(2,128)(2,1)} %bitcast.18, bf16[256,4,2,128]{3,2,1,0:T(2,128)(2,1)} %bitcast.15, ...), custom_call_target="tpu_custom_call" | custom-call | tf_op jit(solution)/shard_map/pallas_call | solution.py:468
  51.1 1.0 %shard_map.86 = (bf16[256,4,2,128]{3,2,1,0:T(2,128)(2,1)}, bf16[256,2,2,128]{3,2,1,0:T(2,128)(2,1)}, bf16[256,2,2,128]{3,2,1,0:T(2,128)(2,1)}) custom-call(bf16[4,256,2,128]{3,2,1,0:T(2,128)(2,1)S(1)} %bitcast.11, bf16[2,256,2,128]{3,2,1,0:T(2,128)(2,1)S(1)} %bitcast.12, bf16[2,256,2,128]{3,2,1,0:T(2,128)(2,1)S(1)} %bitcast.13), custom_call_target="tpu_custom_call" | custom-call | tf_op jit(solution)/shard_map/pallas_call | solution.py:494

commit v3 on v2

--- a/solution.py
+++ b/solution.py
@@ -20,9 +20,9 @@
 NU = 2 * NC
 FAR = 1e30
 VMEM_KIB = 24 << 10
-DIRECT_KV = ()
-DIRECT_G = (3,)
-PLAN = ('flip0', 'A0', 'A1', 'o2', 'X', 'flip1', 'L0', 'N0', 'F0', 'A2', 'A3', 'o3', 'N1', 'L1', 'S0', 'F1', 'A4', 'A5', 'LF', 'S1', 'F2', 'A6', 'A7', 'N2', 'N3', 'S3', 'F3', 'S2', 'Q', 'Z0', 'Z1', 'Z2', 'Z3', 'D', 'Z4', 'Z5', 'Z6', 'Z7')
+VIA = 3
+DIRECT_G = ()
+PLAN = ('A0', 'A1', 'V', 'flip0', 'L0', 'X', 'flip1', 'N0', 'A2', 'F0', 'A3', 'N1', 'A4', 'F3', 'F1', 'S0', 'A5', 'L1', 'N2', 'A6', 'S1', 'F2', 'A7', 'N3', 'S3', 'LF', 'D', 'S2', 'Q', 'Z0', 'Z1', 'Z2', 'Z3', 'Z6', 'Z7', 'Z4', 'Z5')
 
 
 def dot_nt(a, b):
@@ -41,10 +41,10 @@
     n,
     q_hbm, k_hbm, v_hbm, o_hbm, g_hbm, lse_hbm,
     gq_out, gk_out, gv_out,
-    kin, kraw, kv_x, qraw, graw, ob, qf, gf, qt, gt, qx, gx, lse_s, st, stx, kf,
+    kin, kraw, kv_x, via_b, qraw, graw, ob, qf, gf, qt, gt, qx, gx, lse_s, st, stx, kf,
     acc_h, acc_l, dq_t, dqs, g2s, g2r, g1s, g1r, g2d, g0r, fi, fo,
     kv_ld, in_ld,
-    o_send, o_recv, r_send, r_recv, g2_send, g2_recv, g1_send, g1_recv, gd_send, gd_recv,
+    o_send, o_recv, via_send, via_recv, r_send, r_recv, g2_send, g2_recv, g1_send, g1_recv, gd_send, gd_recv,
     x_send, x_recv, dq_send, dq_recv, out_sem,
 ):
     me = lax.axis_index("seq")
@@ -55,6 +55,11 @@
     down = lax.rem(me - k + n - 2, n)
     up2 = lax.rem(me - k + 4, n)
     down2 = lax.rem(me - k + n - 4, n)
+    up3 = lax.rem(me - k + 6, n)
+    down3 = lax.rem(me - k + n - 6, n)
+    y = lax.rem(chip, 4)
+    via_dev = jnp.where(y == 0, up3, down)
+    onward = jnp.where(y == 3, down, up3)
     partner = me - k + oth
 
     def remote(src, dst, ssem, rsem, dev):
@@ -90,9 +95,9 @@
         c.start()
 
     bar = pltpu.get_barrier_semaphore()
-    for dev in (up, up + 1, down, down + 1, up2, up2 + 1, down2, down2 + 1, partner):
+    for dev in (up, up + 1, down, down + 1, up2, up2 + 1, down2, down2 + 1, up3, up3 + 1, down3, down3 + 1, partner):
         pl.semaphore_signal(bar, inc=1, device_id=(dev,), device_id_type=MESH)
-    pl.semaphore_wait(bar, 9)
+    pl.semaphore_wait(bar, 13)
 
     def own_copy(u):
         m = u // 2
@@ -105,10 +110,17 @@
         x = par(u)
         return remote(kraw.at[2 + x, m], kraw.at[2 + x, m], o_send.at[u], o_recv.at[x, m], up)
 
-    def direct_copy(u):
-        m = u // 2
-        src = kraw.at[4 + k, m] if u % 2 == 0 else kv_x.at[m]
-        return remote(src, kraw.at[k, m], r_send.at[u], r_recv.at[k, m], up2 + par(u))
+    def via_copy(u):
+        src = kraw.at[4 + k, VIA] if u % 2 == 0 else kv_x.at[VIA]
+        return remote(src, via_b.at[k], via_send.at[u % 2], via_recv.at[k], via_dev + par(u))
+
+    def via_onward(u):
+        x = par(u)
+        return remote(via_b.at[x], kraw.at[x, VIA], r_send.at[u], r_recv.at[x, VIA], onward + k)
+
+    def via_arrival(u):
+        x = par(u)
+        return remote(via_b.at[x], via_b.at[x], via_send.at[u % 2], via_recv.at[x], via_dev)
 
     def relay_copy(u):
         m = u // 2
@@ -157,11 +169,13 @@
                 for j in range(2):
                     dst[e, j] = kf[e, pl.ds(j, TC, stride=2), :].astype(BF)
 
-    for m in range(NC):
+    for m in (0, VIA, 1, 2):
         split(m)
-        if m < 2:
-            own_copy(2 * m).start()
-            own_copy(2 * m + 1).start()
+        for u in (2 * m, 2 * m + 1):
+            if m == 0:
+                own_copy(u).start()
+            elif m == VIA:
+                via_copy(u).start()
     x_kv.start()
     for raw, near, far, first, copy in ((qraw, qf, qx, 0, x_q), (graw, gf, gx, 4, x_g)):
         for j in range(2):
@@ -330,12 +344,15 @@
 
     def arrive(u):
         own_arrival(u).wait_recv()
-        if u // 2 not in DIRECT_KV:
+        if u // 2 != VIA:
             relay_copy(u).start()
-
-    def own_send(m):
-        own_copy(2 * m).start()
-        own_copy(2 * m + 1).start()
+        if u + 2 < NU:
+            own_copy(u + 2).start()
+
+    def pass_on():
+        for u in (2 * VIA, 2 * VIA + 1):
+            via_arrival(u).wait_recv()
+            via_onward(u).start()
 
     def far_step(m):
         relay_copy(2 * m).wait_recv()
@@ -380,9 +397,9 @@
     steps = {
         "flip0": lambda: flip(k), "flip1": lambda: flip(oth),
         "L0": lambda: local_causal(k), "L1": lambda: local_causal(oth), "LF": local_rest,
-        "X": from_partner, "Q": lambda: g0_copy.wait_recv(), "D": query_grads,
+        "X": from_partner, "V": pass_on, "Q": lambda: g0_copy.wait_recv(), "D": query_grads,
     }
-    by_index = {"A": arrive, "o": own_send, "N": near, "F": far_step, "S": near_step, "Z": final_step}
+    by_index = {"A": arrive, "N": near, "F": far_step, "S": near_step, "Z": final_step}
     for word in PLAN:
         if word in steps:
             steps[word]()
@@ -391,7 +408,9 @@
 
     for u in range(NU):
         own_copy(u).wait_send()
-        (direct_copy if u // 2 in DIRECT_KV else relay_copy)(u).wait_send()
+        (via_onward if u // 2 == VIA else relay_copy)(u).wait_send()
+        if u // 2 == VIA:
+            via_copy(u).wait_send()
         g1_copy(u).wait_send()
         if u // 2 in DIRECT_G:
             g2d_copy(u).wait_send()
@@ -429,6 +448,7 @@
         vm((2, NC, 2, TC, 2, HD), BF),
         vm((6, NC, 2, 2, TC, HD), BF),
         vm((NC, 2, 2, TC, HD), BF),
+        vm((2, 2, 2, TC, HD), BF),
         vm((2, 2) + pair, BF),
         vm((2, 2) + pair, BF),
         vm((2, 2) + pair, BF),
@@ -457,6 +477,7 @@
         dma((NC, 2, 2)),
         dma((13,)),
         dma((NU,)), dma((2, NC)),
+        dma((2,)), dma((2,)),
         dma((NU,)), dma((2, NC)),
         dma((NC, 2)), dma((NC, 2)),
         dma((NU,)), dma((2, NC)),

time: 52.3 us -> 50.1 us (0.958)
  Pallas kernels: 51.5 us -> 49.4 us
    pallas_call x1, Pallas kernels: 50.5 us -> 48.4 us  [shards(): pl.pallas_call(functools.partial(kernel, n), out_shape=(jax.ShapeDtypeStr...]
where the time goes in v3:
time: 50.1 us; the launch traced here: 50 us
  Pallas kernels  49.4 us (99%)
  between operations  0.64 us (1%)
    pallas_call x1, Pallas kernels, shards(): pl.pallas_call(functools.partial(kernel, n), out_shape=(jax.ShapeDtypeStr...  48.4 us
    pallas_call x1, Pallas kernels, shards(): pl.pallas_call(deliver, out_shape=tuple((jax.ShapeDtypeStruct(shape, BF)...  1.03 us

profile of v3, /device:TPU:1, one launch (start us, length us, event | category | flops | bytes accessed | tf_op | source)
XLA Modules:
  0.0 50.0 jit_solution(13947784788454604551)
XLA Ops:
  0.6 48.4 %shard_map.85 = (bf16[4,512,128]{2,1,0:T(8,128)(2,1)S(1)}, bf16[2,512,128]{2,1,0:T(8,128)(2,1)S(1)}, bf16[2,512,128]{2,1,0:T(8,128)(2,1)S(1)}) custom-call(bf16[256,4,2,128]{3,2,1,0:T(2,128)(2,1)} %bitcast.14, bf16[256,2,2,128]{3,2,1,0:T(2,128)(2,1)} %bitcast.17, bf16[256,2,2,128]{3,2,1,0:T(2,128)(2,1)} %bitcast.18, bf16[256,4,2,128]{3,2,1,0:T(2,128)(2,1)} %bitcast.15, ...), custom_call_target="tpu_custom_call" | custom-call | tf_op jit(solution)/shard_map/pallas_call | solution.py:489
  49.0 1.0 %shard_map.86 = (bf16[256,4,2,128]{3,2,1,0:T(2,128)(2,1)}, bf16[256,2,2,128]{3,2,1,0:T(2,128)(2,1)}, bf16[256,2,2,128]{3,2,1,0:T(2,128)(2,1)}) custom-call(bf16[4,256,2,128]{3,2,1,0:T(2,128)(2,1)S(1)} %bitcast.11, bf16[2,256,2,128]{3,2,1,0:T(2,128)(2,1)S(1)} %bitcast.12, bf16[2,256,2,128]{3,2,1,0:T(2,128)(2,1)S(1)} %bitcast.13), custom_call_target="tpu_custom_call" | custom-call | tf_op jit(solution)/shard_map/pallas_call | solution.py:515

commit v4 on v3

--- a/solution.py
+++ b/solution.py
@@ -21,8 +21,11 @@
 FAR = 1e30
 VMEM_KIB = 24 << 10
 VIA = 3
-DIRECT_G = ()
-PLAN = ('A0', 'A1', 'V', 'flip0', 'L0', 'X', 'flip1', 'N0', 'A2', 'F0', 'A3', 'N1', 'A4', 'F3', 'F1', 'S0', 'A5', 'L1', 'N2', 'A6', 'S1', 'F2', 'A7', 'N3', 'S3', 'LF', 'D', 'S2', 'Q', 'Z0', 'Z1', 'Z2', 'Z3', 'Z6', 'Z7', 'Z4', 'Z5')
+PLAN = (
+    "G", "T", "A0", "A1", "V", "flip0", "L0", "X", "flip1", "N0", "A2", "F0", "A3", "N1",
+    "A4", "F3", "F1", "S0", "A5", "L1", "N2", "A6", "S1", "F2", "A7", "N3", "S3", "LF",
+    "D", "S2", "Q", "Z0", "Z1", "Z2", "Z3", "Z6", "Z7", "Z4", "Z5",
+)
 
 
 def dot_nt(a, b):
@@ -42,9 +45,9 @@
     q_hbm, k_hbm, v_hbm, o_hbm, g_hbm, lse_hbm,
     gq_out, gk_out, gv_out,
     kin, kraw, kv_x, via_b, qraw, graw, ob, qf, gf, qt, gt, qx, gx, lse_s, st, stx, kf,
-    acc_h, acc_l, dq_t, dqs, g2s, g2r, g1s, g1r, g2d, g0r, fi, fo,
+    acc_h, acc_l, dq_t, dqs, g2s, g2r, g1s, g1r, g0r, fi, fo,
     kv_ld, in_ld,
-    o_send, o_recv, via_send, via_recv, r_send, r_recv, g2_send, g2_recv, g1_send, g1_recv, gd_send, gd_recv,
+    o_send, o_recv, via_send, via_recv, r_send, r_recv, g2_send, g2_recv, g1_send, g1_recv,
     x_send, x_recv, dq_send, dq_recv, out_sem,
 ):
     me = lax.axis_index("seq")
@@ -53,8 +56,6 @@
     chip = lax.div(me, 2)
     up = lax.rem(me - k + 2, n)
     down = lax.rem(me - k + n - 2, n)
-    up2 = lax.rem(me - k + 4, n)
-    down2 = lax.rem(me - k + n - 4, n)
     up3 = lax.rem(me - k + 6, n)
     down3 = lax.rem(me - k + n - 6, n)
     y = lax.rem(chip, 4)
@@ -70,6 +71,10 @@
 
     def par(u):
         return k if u % 2 == 0 else oth
+
+    bar = pltpu.get_barrier_semaphore()
+    for dev in (up, up + 1, down, down + 1, up3, up3 + 1, down3, down3 + 1, partner):
+        pl.semaphore_signal(bar, inc=1, device_id=(dev,), device_id_type=MESH)
 
     kv_loads = []
     for m in range(NC):
@@ -79,8 +84,9 @@
                 kv_loads.append(
                     pltpu.make_async_copy(src.at[rows, pair], kin.at[i, m, e], kv_ld.at[m, i, e])
                 )
-    for c in kv_loads:
-        c.start()
+    for m in (0, VIA, 1, 2):
+        for c in kv_loads[4 * m : 4 * m + 4]:
+            c.start()
     in_loads = []
     s = 0
     for src, dst2 in ((q_hbm, qraw), (g_hbm, graw), (o_hbm, ob)):
@@ -94,11 +100,6 @@
     for c in in_loads:
         c.start()
 
-    bar = pltpu.get_barrier_semaphore()
-    for dev in (up, up + 1, down, down + 1, up2, up2 + 1, down2, down2 + 1, up3, up3 + 1, down3, down3 + 1, partner):
-        pl.semaphore_signal(bar, inc=1, device_id=(dev,), device_id_type=MESH)
-    pl.semaphore_wait(bar, 13)
-
     def own_copy(u):
         m = u // 2
         src = kraw.at[4 + k, m] if u % 2 == 0 else kv_x.at[m]
@@ -130,14 +131,6 @@
     def g2_copy(m, j):
         return remote(g2s.at[m, j], g2r.at[m, j], g2_send.at[m, j], g2_recv.at[m, j], down + k)
 
-    def g2d_copy(u):
-        m, x = u // 2, par(u)
-        return remote(g2s.at[m, :, x], g2d.at[k, m], gd_send.at[u], gd_recv.at[k, m], down2 + x)
-
-    def g2d_arrival(u):
-        m, p = u // 2, par(u)
-        return remote(g2s.at[m, :, p], g2d.at[p, m], gd_send.at[u], gd_recv.at[p, m], down2)
-
     def g1_copy(u):
         m = u // 2
         x = par(u)
@@ -161,74 +154,78 @@
     def flat(val):
         return val.reshape(val.shape[0] * 2, HD)
 
-    def split(m):
+    def split(m, send=None):
         for i, dst in enumerate((kraw.at[4 + k, m], kv_x.at[m])):
             kv_wait(m, i)
             for e in range(2):
                 kf[e] = flat(kin[i, m, e]).astype(F32)
                 for j in range(2):
                     dst[e, j] = kf[e, pl.ds(j, TC, stride=2), :].astype(BF)
-
-    for m in (0, VIA, 1, 2):
-        split(m)
-        for u in (2 * m, 2 * m + 1):
-            if m == 0:
-                own_copy(u).start()
-            elif m == VIA:
-                via_copy(u).start()
+            if send is not None:
+                send(2 * m + i).start()
+
+    split(0)
+    pl.semaphore_wait(bar, 9)
+    own_copy(0).start()
+    own_copy(1).start()
+    split(VIA, via_copy)
+    split(1)
+    split(2)
     x_kv.start()
-    for raw, near, far, first, copy in ((qraw, qf, qx, 0, x_q), (graw, gf, gx, 4, x_g)):
+    def rows_of_queries():
+        for raw, near, far, first, copy in ((qraw, qf, qx, 0, x_q), (graw, gf, gx, 4, x_g)):
+            for j in range(2):
+                in_loads[first + 2 + j].wait()
+                far[j] = flat(raw[1, j])
+            copy.start()
+            for j in range(2):
+                in_loads[first + j].wait()
+                near[k, j] = flat(raw[0, j])
+
+    def statistics():
+        for i in range(8, 13):
+            in_loads[i].wait()
+        lse = lse_s[...] * LOG2E
+        hi = lse.astype(BF)
+        rest = lse - hi.astype(F32)
+        mid = rest.astype(BF)
+        low = (rest - mid.astype(F32)).astype(BF)
+        parts = jnp.concatenate([hi.astype(F32), mid.astype(F32), low.astype(F32), jnp.zeros_like(lse)], 0).astype(BF)
+        row = lax.broadcasted_iota(jnp.int32, (T, 2 * T), 0)
+        col = lax.broadcasted_iota(jnp.int32, (T, 2 * T), 1)
+        wide = []
+        for e in range(2):
+            place = jnp.where(col == 2 * row + e, 1.0, 0.0).astype(BF)
+            r = dot_nn(parts, place)
+            wide.append(r[0:8] + r[8:16] + r[16:24])
+        lse_w = [wide[0][2 * i : 2 * i + 1] + wide[1][2 * i + 1 : 2 * i + 2] for i in range(4)]
+        ones = jnp.ones((8, HD), BF)
+
+        def delta_of(a, b):
+            prod = a.astype(F32) * b.astype(F32)
+            top = prod.astype(BF)
+            left = (prod - top.astype(F32)).astype(BF)
+            return (dot_nt(ones, top) + dot_nt(ones, left))[0:1]
+
+        no_1 = jnp.where(chip < 1, FAR, 0.0).astype(F32)
+        no_2 = jnp.where(chip < 2, FAR, 0.0).astype(F32)
         for j in range(2):
-            in_loads[first + 2 + j].wait()
-            far[j] = flat(raw[1, j])
-        copy.start()
-        for j in range(2):
-            in_loads[first + j].wait()
-            near[k, j] = flat(raw[0, j])
-    for i in range(8, 13):
-        in_loads[i].wait()
-
-    lse = lse_s[...] * LOG2E
-    hi = lse.astype(BF)
-    rest = lse - hi.astype(F32)
-    mid = rest.astype(BF)
-    low = (rest - mid.astype(F32)).astype(BF)
-    parts = jnp.concatenate([hi.astype(F32), mid.astype(F32), low.astype(F32), jnp.zeros_like(lse)], 0).astype(BF)
-    row = lax.broadcasted_iota(jnp.int32, (T, 2 * T), 0)
-    col = lax.broadcasted_iota(jnp.int32, (T, 2 * T), 1)
-    wide = []
-    for e in range(2):
-        place = jnp.where(col == 2 * row + e, 1.0, 0.0).astype(BF)
-        r = dot_nn(parts, place)
-        wide.append(r[0:8] + r[8:16] + r[16:24])
-    lse_w = [wide[0][2 * i : 2 * i + 1] + wide[1][2 * i + 1 : 2 * i + 2] for i in range(4)]
-    ones = jnp.ones((8, HD), BF)
-
-    def delta_of(a, b):
-        prod = a.astype(F32) * b.astype(F32)
-        top = prod.astype(BF)
-        left = (prod - top.astype(F32)).astype(BF)
-        return (dot_nt(ones, top) + dot_nt(ones, left))[0:1]
-
-    no_1 = jnp.where(chip < 1, FAR, 0.0).astype(F32)
-    no_2 = jnp.where(chip < 2, FAR, 0.0).astype(F32)
-    for j in range(2):
-        for which in range(2):
-            if which == 0:
-                dst, dl = st.at[k, j], delta_of(gf[k, j], flat(ob[0, j]))
-            else:
-                dst, dl = stx.at[j], delta_of(gx[j], flat(ob[1, j]))
-            if which == 0:
-                lw = jnp.where(k == 0, lse_w[j], lse_w[2 + j])
-            else:
-                lw = jnp.where(k == 0, lse_w[2 + j], lse_w[j])
-            dst[0:1, :] = lw
-            dst[1:2, :] = dl
-            dst[2:3, :] = lw + no_1
-            dst[3:4, :] = lw + no_2
-            dst[4:8, :] = jnp.zeros((4, 2 * T), F32)
-    x_st.start()
-    dq_t[...] = jnp.zeros_like(dq_t)
+            for which in range(2):
+                if which == 0:
+                    dst, dl = st.at[k, j], delta_of(gf[k, j], flat(ob[0, j]))
+                else:
+                    dst, dl = stx.at[j], delta_of(gx[j], flat(ob[1, j]))
+                if which == 0:
+                    lw = jnp.where(k == 0, lse_w[j], lse_w[2 + j])
+                else:
+                    lw = jnp.where(k == 0, lse_w[2 + j], lse_w[j])
+                dst[0:1, :] = lw
+                dst[1:2, :] = dl
+                dst[2:3, :] = lw + no_1
+                dst[3:4, :] = lw + no_2
+                dst[4:8, :] = jnp.zeros((4, 2 * T), F32)
+        x_st.start()
+        dq_t[...] = jnp.zeros_like(dq_t)
 
     def flip(b):
         for j in range(2):
@@ -306,20 +303,17 @@
             g2s[m, j, 0, 1] = dv0[:TC].astype(BF)
             g2s[m, j, 1, 0] = (dk0[TC:] + dk1).astype(BF)
             g2s[m, j, 1, 1] = (dv0[TC:] + dv1).astype(BF)
-            if m not in DIRECT_G:
-                g2_copy(m, j).start()
+            g2_copy(m, j).start()
 
         heads(body)
 
     def near_finish(m):
         for j in range(2):
-            if m not in DIRECT_G:
-                g2_copy(m, j).wait_recv()
+            g2_copy(m, j).wait_recv()
             for x in range(2):
                 for e in range(2):
                     val = acc_h[m, e, j, x * TC : (x + 1) * TC]
-                    if m not in DIRECT_G:
-                        val = val + g2r[m, j, x, e].astype(F32)
+                    val = val + g2r[m, j, x, e].astype(F32)
                     g1s[m, x, e, j] = val.astype(BF)
 
     outs = []
@@ -331,8 +325,6 @@
             for j in range(2):
                 mine = acc_l[k, e, j, rows, :] if u % 2 == 0 else g0r[e, j, rows, :]
                 val = mine + g1r[p, m, e, j].astype(F32)
-                if m in DIRECT_G:
-                    val = val + g2d[p, m, j, e].astype(F32)
                 if e == 0:
                     val = val * SCALE
                 fi[e, pl.ds(j, TC, stride=2), :] = val
@@ -358,9 +350,6 @@
         relay_copy(2 * m).wait_recv()
         relay_copy(2 * m + 1).wait_recv()
         far(m)
-        if m in DIRECT_G:
-            g2d_copy(2 * m).start()
-            g2d_copy(2 * m + 1).start()
 
     def near_step(m):
         near_finish(m)
@@ -369,8 +358,6 @@
 
     def final_step(u):
         g1_arrival(u).wait_recv()
-        if u // 2 in DIRECT_G:
-            g2d_arrival(u).wait_recv()
         final_unit(u)
 
     def from_partner():
@@ -397,7 +384,7 @@
     steps = {
         "flip0": lambda: flip(k), "flip1": lambda: flip(oth),
         "L0": lambda: local_causal(k), "L1": lambda: local_causal(oth), "LF": local_rest,
-        "X": from_partner, "V": pass_on, "Q": lambda: g0_copy.wait_recv(), "D": query_grads,
+        "X": from_partner, "G": rows_of_queries, "T": statistics, "V": pass_on, "Q": lambda: g0_copy.wait_recv(), "D": query_grads,
     }
     by_index = {"A": arrive, "N": near, "F": far_step, "S": near_step, "Z": final_step}
     for word in PLAN:
@@ -412,12 +399,9 @@
         if u // 2 == VIA:
             via_copy(u).wait_send()
         g1_copy(u).wait_send()
-        if u // 2 in DIRECT_G:
-            g2d_copy(u).wait_send()
     for m in range(NC):
-        if m not in DIRECT_G:
-            for j in range(2):
-                g2_copy(m, j).wait_send()
+        for j in range(2):
+            g2_copy(m, j).wait_send()
     for c in (x_kv, x_q, x_g, x_st, g0_copy):
         c.wait_send()
     for c in dq_copies:
@@ -470,7 +454,6 @@
         vm((NC, 2, 2, 2, TC, HD), BF),
         vm((NC, 2, 2, 2, TC, HD), BF),
         vm((2, NC, 2, 2, TC, HD), BF),
-        vm((2, NC, 2, 2, TC, HD), BF),
         vm((2, 2, T, HD), F32),
         vm((2, 2 * TC, HD), F32),
         vm((NU, 2, 2 * TC, HD), BF),
@@ -480,7 +463,6 @@
         dma((2,)), dma((2,)),
         dma((NU,)), dma((2, NC)),
         dma((NC, 2)), dma((NC, 2)),
-        dma((NU,)), dma((2, NC)),
         dma((NU,)), dma((2, NC)),
         dma((5,)), dma((5,)),
         dma((2,)), dma((2,)),

time: 50.1 us -> 49.8 us (level)
  no operation moved by 1% of the time
where the time goes in v4:
time: 49.8 us; the launch traced here: 49.7 us
  Pallas kernels  49.1 us (99%)
  between operations  0.64 us (1%)
    pallas_call x1, Pallas kernels, shards(): pl.pallas_call(functools.partial(kernel, n), out_shape=(jax.ShapeDtypeStr...  48.1 us
    pallas_call x1, Pallas kernels, shards(): pl.pallas_call(deliver, out_shape=tuple((jax.ShapeDtypeStruct(shape, BF)...  1.03 us

profile of v4, /device:TPU:1, one launch (start us, length us, event | category | flops | bytes accessed | tf_op | source)
XLA Modules:
  0.0 49.7 jit_solution(11405907995993365365)
XLA Ops:
  0.6 48.1 %shard_map.85 = (bf16[4,512,128]{2,1,0:T(8,128)(2,1)S(1)}, bf16[2,512,128]{2,1,0:T(8,128)(2,1)S(1)}, bf16[2,512,128]{2,1,0:T(8,128)(2,1)S(1)}) custom-call(bf16[256,4,2,128]{3,2,1,0:T(2,128)(2,1)} %bitcast.14, bf16[256,2,2,128]{3,2,1,0:T(2,128)(2,1)} %bitcast.17, bf16[256,2,2,128]{3,2,1,0:T(2,128)(2,1)} %bitcast.18, bf16[256,4,2,128]{3,2,1,0:T(2,128)(2,1)} %bitcast.15, ...), custom_call_target="tpu_custom_call" | custom-call | tf_op jit(solution)/shard_map/pallas_call | solution.py:471
  48.7 1.0 %shard_map.86 = (bf16[256,4,2,128]{3,2,1,0:T(2,128)(2,1)}, bf16[256,2,2,128]{3,2,1,0:T(2,128)(2,1)}, bf16[256,2,2,128]{3,2,1,0:T(2,128)(2,1)}) custom-call(bf16[4,256,2,128]{3,2,1,0:T(2,128)(2,1)S(1)} %bitcast.11, bf16[2,256,2,128]{3,2,1,0:T(2,128)(2,1)S(1)} %bitcast.12, bf16[2,256,2,128]{3,2,1,0:T(2,128)(2,1)S(1)} %bitcast.13), custom_call_target="tpu_custom_call" | custom-call | tf_op jit(solution)/shard_map/pallas_call | solution.py:497
